TPU v7x, 768 devices: a whole 4x8x12 slice. The times are simulated.
768 devices in a mesh: slot: 6 (over z_lo), tile: 8 (over z_hi, x), obs: 16 (over y, core).
Axes of the slice: x: 4, y: 8, z: 12 (z_hi: 2, z_lo: 6; z = z_hi * 6 + z_lo), core: 2. Of those that a mesh axis runs over, the one named last changes fastest.
Arguments:
- forcing: float32 [6, 128, 64, 2048], P('slot', None, 'tile', 'obs'), may hold values from -6 to 6
- winds: float32 [2, 6, 64, 2048], P(None, 'slot', 'tile', 'obs'), may hold values from -0.2 to 0.2
- mixing: float32 [128, 128], replicated, may hold values from -0.12 to 0.12
- observation_columns: int32 [4, 6, 262144], P(None, 'slot', ('tile', 'obs')), may hold values from 0 to 1023
- obs_weights: float32 [4, 6, 262144], P(None, 'slot', ('tile', 'obs')), may hold values from 0.05 to 0.5
- obs_counts: int32 [6, 128, 16], P('slot', ('tile', 'obs')), may hold values from 16 to 128, as said below
- jacobian: float32 [6, 16, 128, 128], P('slot', 'obs'), may hold values from -0.5 to 0.5
Outputs:
- states: float32 [6, 128, 64, 2048], P('slot', None, 'tile', 'obs')
- radiances: float32 [6, 128, 262144], P('slot', None, ('tile', 'obs'))
Inputs may be any that keep to these rules, and one draw needn't show every extreme that they name: `obs_counts`: every block of 128 rows has its live rows first; in every slot and every tile one owner's blocks are full from every source.
All inputs are finite; a program needn't handle non-finite values.
Results may differ from a plain program's by a relative error of at most 0.0001.
Values sent between devices are 32-bit elements; how exact they have to be, the bound alone decides.
No kernel may reach another device: no remote copies, remote signals or barrier semaphores. Data moves between devices by JAX's collectives and lax.ppermute only.
A program may use at most 32 MiB of HBM per device.

v0:
```python
import jax
import jax.numpy as jnp
from jax import lax
from jax.sharding import PartitionSpec as P

STEPS = 4


mixing_rate = 0.15


def padded_2(block, sides, width):
    for axis, dim in sides:
        count = lax.axis_size(axis)
        forward = [(i, i + 1) for i in range(count - 1)]
        forward.append((count - 1, 0))
        backward = [(target, source) for source, target in forward]
        low = lax.ppermute(
            lax.slice_in_dim(block, block.shape[dim] - width, None, axis=dim), axis, forward
        )
        high = lax.ppermute(lax.slice_in_dim(block, 0, width, axis=dim), axis, backward)
        block = jnp.concatenate([low, block, high], axis=dim)
    return block


def passed_along(x, axis, by):
    size = lax.axis_size(axis)
    pairs = [(i, i + by) for i in range(size) if 0 <= i + by < size]
    return lax.ppermute(x, axis, pairs)


def advance_slot(padded, eastward_rate, northward_rate, mixing):
    centre = padded[:, 1:-1, 1:-1]
    eastern = padded[:, 2:, 1:-1]
    western = padded[:, :-2, 1:-1]
    northern = padded[:, 1:-1, 2:]
    southern = padded[:, 1:-1, :-2]
    shifted_state = (
        centre + eastward_rate * (eastern - western) + northward_rate * (northern - southern)
    )
    shifted_state = shifted_state + mixing_rate * (
        eastern + western + northern + southern - 4.0 * centre
    )
    return shifted_state + jnp.einsum(
        "mn,nlk->mlk", mixing, shifted_state, precision=lax.Precision.HIGHEST
    )


def local(forcing, winds, mixing, observation_columns, obs_weights, obs_counts, jacobian):
    source = forcing[0]
    current = source
    rates = winds[:, 0]
    rounds = lax.axis_size("slot") - 1
    width_x = current.shape[1]
    width_y = current.shape[2]
    broad_rates = padded_2(rates, (("tile", 1), ("obs", 2)), STEPS)
    for round_index in range(rounds):
        padded = padded_2(current, (("tile", 1), ("obs", 2)), STEPS)
        for step in range(STEPS):
            margin = STEPS - step - 1
            lower = step + 1
            window = broad_rates[
                :, lower : lower + width_x + 2 * margin, lower : lower + width_y + 2 * margin
            ]
            padded = advance_slot(padded, window[0], window[1], mixing)
        current = padded
        current = passed_along(current, "slot", 1) + source
    levels = current.shape[0]
    flat = current.reshape(levels, width_x * width_y)
    cells = observation_columns[:, 0]
    weights = obs_weights[:, 0]
    profile = weights[0] * jnp.take(flat, cells[0], axis=1)
    for corner in range(1, 4):
        profile = profile + weights[corner] * jnp.take(flat, cells[corner], axis=1)
    owners = obs_counts.shape[2]
    capacity = cells.shape[1] // owners
    live = (jnp.arange(capacity, dtype=jnp.int32)[None, :] < obs_counts[0, 0][:, None]).astype(
        jnp.float32
    )
    profile = profile.reshape(levels, owners, capacity) * live[None]
    table = jacobian[0, 0]
    radiance = jnp.einsum(
        "cv,vsk->csk",
        table,
        lax.all_to_all(profile, "obs", split_axis=1, concat_axis=1, tiled=True),
        precision=lax.Precision.HIGHEST,
    )
    return (current[None], radiance.reshape(1, table.shape[0], owners * capacity))


def solution(mesh):
    return jax.shard_map(
        local,
        mesh=mesh,
        in_specs=(
            P("slot", None, "tile", "obs"),
            P(None, "slot", "tile", "obs"),
            P(),
            P(None, "slot", ("tile", "obs")),
            P(None, "slot", ("tile", "obs")),
            P("slot", ("tile", "obs"), None),
            P("slot", "obs", None, None),
        ),
        out_specs=(P("slot", None, "tile", "obs"), P("slot", None, ("tile", "obs"))),
        check_vma=False,
    )
```

profile of v0, /device:TPU:1, one launch (start us, length us, event | category | flops | bytes accessed | tf_op | source)
XLA Modules:
  0.0 402.7 jit_solution(4630015843095403940)
XLA Ops:
  1.5 3.9 collective-permute-start.4
  5.4 15.9 %collective-permute-start.5 = (f32[2,4,128]{2,1,0:T(4,128)S(1)}, f32[2,4,128]{2,1,0:T(4,128)S(1)}, u32[]{:S(2)}, u32[]{:S(2)}) collective-permute-start(f32[2,4,128]{2,1,0:T(4,128)S(1)} %get-tuple-element.44), channel_id=1, source_target_pairs={{16,0},{32,16},{48,32},{64,48},{80,64},{96,80},{112,96},{0,112},{1... | collective-permute-start | bytes 12296 | tf_op jit(solution)/shard_map/ppermute | solution.py:21
  24.5 11.8 %collective-permute-start.1 = (f32[128,4,128]{0,2,1:T(8,128)S(1)}, f32[128,4,128]{0,2,1:T(8,128)S(1)}, u32[]{:S(2)}, u32[]{:S(2)}) collective-permute-start(f32[128,4,128]{0,2,1:T(8,128)S(1)} %get-tuple-element.24), channel_id=1, source_target_pairs={{16,0},{32,16},{48,32},{64,48},{80,64},{96,80},{112,96},{0,112},{1... | collective-permute-start | bytes 786440 | tf_op jit(solution)/shard_map/ppermute | solution.py:21
  39.1 2.8 collective-permute-start.7
  55.8 14.2 %collective-permute-start.8 = (f32[128,8,128]{0,2,1:T(8,128)S(1)}, f32[128,8,128]{0,2,1:T(8,128)S(1)}, u32[]{:S(2)}, u32[]{:S(2)}) collective-permute-start(f32[128,8,128]{0,2,1:T(8,128)S(1)} %fusion.19), channel_id=1, source_target_pairs={{0,128},{128,256},{256,384},{384,512},{512,640},{1,129},{129,257},... | collective-permute-start | bytes 1572872 | tf_op jit(solution)/shard_map/ppermute | solution.py:29
  70.0 11.2 %collective-permute-done.8 = f32[128,8,128]{0,2,1:T(8,128)S(1)} collective-permute-done((f32[128,8,128]{0,2,1:T(8,128)S(1)}, f32[128,8,128]{0,2,1:T(8,128)S(1)}, u32[]{:S(2)}, u32[]{:S(2)}) %collective-permute-start.8) | collective-permute-done | bytes 524320 | tf_op jit(solution)/shard_map/ppermute | solution.py:29
  81.3 13.3 %collective-permute-start.10 = (f32[128,4,128]{0,2,1:T(8,128)S(1)}, f32[128,4,128]{0,2,1:T(8,128)S(1)}, u32[]{:S(2)}, u32[]{:S(2)}) collective-permute-start(f32[128,4,128]{0,2,1:T(8,128)S(1)} %get-tuple-element.22), channel_id=1, source_target_pairs={{16,0},{32,16},{48,32},{64,48},{80,64},{96,80},{112,96},{0,112},{1... | collective-permute-start | bytes 786440 | tf_op jit(solution)/shard_map/ppermute | solution.py:21
  96.6 2.8 collective-permute-done.10
  99.4 12.3 %collective-permute-done.9 = f32[128,4,128]{0,2,1:T(8,128)S(1)} collective-permute-done((f32[128,4,128]{0,2,1:T(8,128)S(1)}, f32[128,4,128]{0,2,1:T(8,128)S(1)}, u32[]{:S(2)}, u32[]{:S(2)}) %collective-permute-start.9) | collective-permute-done | bytes 262176 | tf_op jit(solution)/shard_map/ppermute | solution.py:18
  111.7 3.2 collective-permute-start.11
  126.5 14.8 %collective-permute-start.13 = (f32[128,8,128]{0,2,1:T(8,128)S(1)}, f32[128,8,128]{0,2,1:T(8,128)S(1)}, u32[]{:S(2)}, u32[]{:S(2)}) collective-permute-start(f32[128,8,128]{0,2,1:T(8,128)S(1)} %fusion.18), channel_id=1, source_target_pairs={{0,128},{128,256},{256,384},{384,512},{512,640},{1,129},{129,257},... | collective-permute-start | bytes 1572872 | tf_op jit(solution)/shard_map/ppermute | solution.py:29
  141.3 10.8 %collective-permute-done.13 = f32[128,8,128]{0,2,1:T(8,128)S(1)} collective-permute-done((f32[128,8,128]{0,2,1:T(8,128)S(1)}, f32[128,8,128]{0,2,1:T(8,128)S(1)}, u32[]{:S(2)}, u32[]{:S(2)}) %collective-permute-start.13) | collective-permute-done | bytes 524320 | tf_op jit(solution)/shard_map/ppermute | solution.py:29
  154.2 11.8 %collective-permute-start.15 = (f32[128,4,128]{0,2,1:T(8,128)S(1)}, f32[128,4,128]{0,2,1:T(8,128)S(1)}, u32[]{:S(2)}, u32[]{:S(2)}) collective-permute-start(f32[128,4,128]{0,2,1:T(8,128)S(1)} %get-tuple-element.20), channel_id=1, source_target_pairs={{16,0},{32,16},{48,32},{64,48},{80,64},{96,80},{112,96},{0,112},{1... | collective-permute-start | bytes 786440 | tf_op jit(solution)/shard_map/ppermute | solution.py:21
  166.0 3.2 collective-permute-done.14
  170.1 3.5 collective-permute-start.16
  185.2 15.1 %collective-permute-start.18 = (f32[128,8,128]{0,2,1:T(8,128)S(1)}, f32[128,8,128]{0,2,1:T(8,128)S(1)}, u32[]{:S(2)}, u32[]{:S(2)}) collective-permute-start(f32[128,8,128]{0,2,1:T(8,128)S(1)} %fusion.17), channel_id=1, source_target_pairs={{0,128},{128,256},{256,384},{384,512},{512,640},{1,129},{129,257},... | collective-permute-start | bytes 1572872 | tf_op jit(solution)/shard_map/ppermute | solution.py:29
  200.4 10.8 %collective-permute-done.18 = f32[128,8,128]{0,2,1:T(8,128)S(1)} collective-permute-done((f32[128,8,128]{0,2,1:T(8,128)S(1)}, f32[128,8,128]{0,2,1:T(8,128)S(1)}, u32[]{:S(2)}, u32[]{:S(2)}) %collective-permute-start.18) | collective-permute-done | bytes 524320 | tf_op jit(solution)/shard_map/ppermute | solution.py:29
  213.3 13.2 %collective-permute-start.20 = (f32[128,4,128]{0,2,1:T(8,128)S(1)}, f32[128,4,128]{0,2,1:T(8,128)S(1)}, u32[]{:S(2)}, u32[]{:S(2)}) collective-permute-start(f32[128,4,128]{0,2,1:T(8,128)S(1)} %get-tuple-element.18), channel_id=1, source_target_pairs={{16,0},{32,16},{48,32},{64,48},{80,64},{96,80},{112,96},{0,112},{1... | collective-permute-start | bytes 786440 | tf_op jit(solution)/shard_map/ppermute | solution.py:21
  226.5 3.5 collective-permute-done.19
  242.6 16.2 %collective-permute-start.23 = (f32[128,8,128]{0,2,1:T(8,128)S(1)}, f32[128,8,128]{0,2,1:T(8,128)S(1)}, u32[]{:S(2)}, u32[]{:S(2)}) collective-permute-start(f32[128,8,128]{0,2,1:T(8,128)S(1)} %fusion.16), channel_id=1, source_target_pairs={{0,128},{128,256},{256,384},{384,512},{512,640},{1,129},{129,257},... | collective-permute-start | bytes 1572872 | tf_op jit(solution)/shard_map/ppermute | solution.py:29
  258.9 9.3 %collective-permute-done.23 = f32[128,8,128]{0,2,1:T(8,128)S(1)} collective-permute-done((f32[128,8,128]{0,2,1:T(8,128)S(1)}, f32[128,8,128]{0,2,1:T(8,128)S(1)}, u32[]{:S(2)}, u32[]{:S(2)}) %collective-permute-start.23) | collective-permute-done | bytes 524320 | tf_op jit(solution)/shard_map/ppermute | solution.py:29
  270.3 12.9 %collective-permute-start.25 = (f32[128,4,128]{0,2,1:T(8,128)S(1)}, f32[128,4,128]{0,2,1:T(8,128)S(1)}, u32[]{:S(2)}, u32[]{:S(2)}) collective-permute-start(f32[128,4,128]{0,2,1:T(8,128)S(1)} %get-tuple-element.16), channel_id=1, source_target_pairs={{16,0},{32,16},{48,32},{64,48},{80,64},{96,80},{112,96},{0,112},{1... | collective-permute-start | bytes 786440 | tf_op jit(solution)/shard_map/ppermute | solution.py:21
  286.5 8.9 %collective-permute-start.26 = (f32[128,16,4]{0,2,1:T(4,128)S(1)}, f32[128,16,4]{0,2,1:T(4,128)S(1)}, u32[]{:S(2)}, u32[]{:S(2)}) collective-permute-start(f32[128,16,4]{0,2,1:T(4,128)S(1)} %get-tuple-element.5), channel_id=1, source_target_pairs={{0,1},{1,2},{2,3},{3,4},{4,5},{5,6},{6,7},{7,8},{8,9},{9,10},{10,1... | collective-permute-start | bytes 98312 | tf_op jit(solution)/shard_map/ppermute | solution.py:18
  307.1 12.1 %collective-permute-start.28 = (f32[128,8,128]{0,2,1:T(8,128)S(1)}, f32[128,8,128]{0,2,1:T(8,128)S(1)}, u32[]{:S(2)}, u32[]{:S(2)}) collective-permute-start(f32[128,8,128]{0,2,1:T(8,128)S(1)} %fusion.15), channel_id=1, source_target_pairs={{0,128},{128,256},{256,384},{384,512},{512,640},{1,129},{129,257},... | collective-permute-start | bytes 1572872 | tf_op jit(solution)/shard_map/ppermute | solution.py:29
  319.4 9.5 %collective-permute-done.28 = f32[128,8,128]{0,2,1:T(8,128)S(1)} collective-permute-done((f32[128,8,128]{0,2,1:T(8,128)S(1)}, f32[128,8,128]{0,2,1:T(8,128)S(1)}, u32[]{:S(2)}, u32[]{:S(2)}) %collective-permute-start.28) | collective-permute-done | bytes 524320 | tf_op jit(solution)/shard_map/ppermute | solution.py:29
  328.9 5.5 %gather_fusion = f32[2048,128]{1,0:T(8,128)S(1)} fusion(f32[128,1024]{0,1:T(8,128)S(1)} %bitcast.185, s32[2048]{0:T(1024)S(1)} %fusion.486), kind=kCustom, calls=%fused_computation.clone | custom fusion | bytes 2105344 | tf_op jit(solution)/shard_map/jit(_take)/gather | solution.py:72
  334.4 5.5 %gather_fusion.1 = f32[2048,128]{1,0:T(8,128)S(1)} fusion(f32[128,1024]{0,1:T(8,128)S(1)} %bitcast.186, s32[2048]{0:T(1024)S(1)} %fusion.487), kind=kCustom, calls=%fused_computation.1.clone | custom fusion | bytes 2105344 | tf_op jit(solution)/shard_map/jit(_take)/gather | solution.py:74
  339.9 7.6 %gather_fusion.2 = f32[2048,128]{1,0:T(8,128)} fusion(f32[128,1024]{0,1:T(8,128)S(1)} %bitcast.187, s32[2048]{0:T(1024)S(1)} %fusion.488), kind=kCustom, calls=%fused_computation.2.clone | custom fusion | bytes 2105344 | tf_op jit(solution)/shard_map/jit(_take)/gather | solution.py:74
  347.5 7.6 %gather_fusion.3 = f32[2048,128]{1,0:T(8,128)} fusion(f32[128,1024]{0,1:T(8,128)S(1)} %bitcast.188, s32[2048]{0:T(1024)S(1)} %fusion.489), kind=kCustom, calls=%fused_computation.3.clone | custom fusion | bytes 2105344 | tf_op jit(solution)/shard_map/jit(_take)/gather | solution.py:74
  355.1 5.8 %fusion.20 = f32[128,2048]{0,1:T(8,128)S(1)} fusion(f32[2048,128]{1,0:T(8,128)} %gather_fusion.3, f32[2048,128]{1,0:T(8,128)} %gather_fusion.2, f32[2048,128]{1,0:T(8,128)S(1)} %gather_fusion.1, f32[2048,128]{1,0:T(8,128)S(1)} %gather_fusion, f32[2048]{0:T(1024)S(1)} %bitcast.208, f32[2048]{0:T(1024)S(1)} %bitcast.209, f32[2048]{0:T(1024)S(1)} %bitcast.207, ...), kind=kLoop, calls=%fused_computation.50 | loop fusion | flops 2883584 | bytes 5283840 | tf_op jit(solution)/shard_map/add | solution.py:74
  362.2 10.1 %all-to-all-start = ((f32[128,16,128]{0,2,1:T(8,128)}), f32[128,16,128]{0,2,1:T(8,128)S(1)}, u32[]{:S(2)}, u32[]{:S(2)}) async-start(f32[128,16,128]{0,2,1:T(8,128)} %broadcast_multiply_fusion), calls=%async_computation | async-start | bytes 2097152 | tf_op jit(solution)/shard_map/all_to_all | solution.py:85
  373.4 27.0 %all-to-all-done = f32[128,16,128]{0,2,1:T(8,128)S(1)} async-done(((f32[128,16,128]{0,2,1:T(8,128)}), f32[128,16,128]{0,2,1:T(8,128)S(1)}, u32[]{:S(2)}, u32[]{:S(2)}) %all-to-all-start) | async-done | bytes 1048608 | tf_op jit(solution)/shard_map/all_to_all | solution.py:85
  (107 shorter events, 85.2 us)
Async XLA Ops:
  0.6 47.0 %copy-start = (f32[128,128]{1,0:T(8,128)S(1)}, f32[128,128]{1,0:T(8,128)}, u32[]{:S(2)}) copy-start(f32[128,128]{1,0:T(8,128)} %param.11) | copy-start | bytes 196612
  1.5 34.8 %collective-permute-start.4 = (f32[2,4,128]{2,1,0:T(4,128)S(1)}, f32[2,4,128]{2,1,0:T(4,128)S(1)}, u32[]{:S(2)}, u32[]{:S(2)}) collective-permute-start(f32[2,4,128]{2,1,0:T(4,128)S(1)} %get-tuple-element.43), channel_id=1, source_target_pairs={{0,16},{16,32},{32,48},{48,64},{64,80},{80,96},{96,112},{112,0},{1... | collective-permute-start | bytes 12296 | tf_op jit(solution)/shard_map/ppermute | solution.py:18
  5.4 30.9 %collective-permute-start.5 = (f32[2,4,128]{2,1,0:T(4,128)S(1)}, f32[2,4,128]{2,1,0:T(4,128)S(1)}, u32[]{:S(2)}, u32[]{:S(2)}) collective-permute-start(f32[2,4,128]{2,1,0:T(4,128)S(1)} %get-tuple-element.44), channel_id=1, source_target_pairs={{16,0},{32,16},{48,32},{64,48},{80,64},{96,80},{112,96},{0,112},{1... | collective-permute-start | bytes 12296 | tf_op jit(solution)/shard_map/ppermute | solution.py:21
  22.5 20.4 %collective-permute-start = (f32[128,4,128]{0,2,1:T(8,128)S(1)}, f32[128,4,128]{0,2,1:T(8,128)S(1)}, u32[]{:S(2)}, u32[]{:S(2)}) collective-permute-start(f32[128,4,128]{0,2,1:T(8,128)S(1)} %get-tuple-element.23), channel_id=1, source_target_pairs={{0,16},{16,32},{32,48},{48,64},{64,80},{80,96},{96,112},{112,0},{1... | collective-permute-start | bytes 786440 | tf_op jit(solution)/shard_map/ppermute | solution.py:18
  24.5 18.5 %collective-permute-start.1 = (f32[128,4,128]{0,2,1:T(8,128)S(1)}, f32[128,4,128]{0,2,1:T(8,128)S(1)}, u32[]{:S(2)}, u32[]{:S(2)}) collective-permute-start(f32[128,4,128]{0,2,1:T(8,128)S(1)} %get-tuple-element.24), channel_id=1, source_target_pairs={{16,0},{32,16},{48,32},{64,48},{80,64},{96,80},{112,96},{0,112},{1... | collective-permute-start | bytes 786440 | tf_op jit(solution)/shard_map/ppermute | solution.py:21
  36.4 6.2 %collective-permute-start.6 = (f32[2,16,4]{2,1,0:T(8,128)S(1)}, f32[2,16,4]{2,1,0:T(8,128)S(1)}, u32[]{:S(2)}, u32[]{:S(2)}) collective-permute-start(f32[2,16,4]{2,1,0:T(8,128)S(1)} %get-tuple-element.39), channel_id=1, source_target_pairs={{0,1},{1,2},{2,3},{3,4},{4,5},{5,6},{6,7},{7,8},{8,9},{9,10},{10,1... | collective-permute-start | bytes 1544 | tf_op jit(solution)/shard_map/ppermute | solution.py:18
  39.1 3.7 collective-permute-start.7
  43.0 4.3 %collective-permute-start.2 = (f32[128,16,4]{0,2,1:T(4,128)S(1)}, f32[128,16,4]{0,2,1:T(4,128)S(1)}, u32[]{:S(2)}, u32[]{:S(2)}) collective-permute-start(f32[128,16,4]{0,2,1:T(4,128)S(1)} %get-tuple-element.13), channel_id=1, source_target_pairs={{0,1},{1,2},{2,3},{3,4},{4,5},{5,6},{6,7},{7,8},{8,9},{9,10},{10,1... | collective-permute-start | bytes 98312 | tf_op jit(solution)/shard_map/ppermute | solution.py:18
  44.0 3.5 collective-permute-start.3
  55.8 25.4 %collective-permute-start.8 = (f32[128,8,128]{0,2,1:T(8,128)S(1)}, f32[128,8,128]{0,2,1:T(8,128)S(1)}, u32[]{:S(2)}, u32[]{:S(2)}) collective-permute-start(f32[128,8,128]{0,2,1:T(8,128)S(1)} %fusion.19), channel_id=1, source_target_pairs={{0,128},{128,256},{256,384},{384,512},{512,640},{1,129},{129,257},... | collective-permute-start | bytes 1572872 | tf_op jit(solution)/shard_map/ppermute | solution.py:29
  81.3 18.1 %collective-permute-start.10 = (f32[128,4,128]{0,2,1:T(8,128)S(1)}, f32[128,4,128]{0,2,1:T(8,128)S(1)}, u32[]{:S(2)}, u32[]{:S(2)}) collective-permute-start(f32[128,4,128]{0,2,1:T(8,128)S(1)} %get-tuple-element.22), channel_id=1, source_target_pairs={{16,0},{32,16},{48,32},{64,48},{80,64},{96,80},{112,96},{0,112},{1... | collective-permute-start | bytes 786440 | tf_op jit(solution)/shard_map/ppermute | solution.py:21
  94.7 17.0 %collective-permute-start.9 = (f32[128,4,128]{0,2,1:T(8,128)S(1)}, f32[128,4,128]{0,2,1:T(8,128)S(1)}, u32[]{:S(2)}, u32[]{:S(2)}) collective-permute-start(f32[128,4,128]{0,2,1:T(8,128)S(1)} %get-tuple-element.21), channel_id=1, source_target_pairs={{0,16},{16,32},{32,48},{48,64},{64,80},{80,96},{96,112},{112,0},{1... | collective-permute-start | bytes 786440 | tf_op jit(solution)/shard_map/ppermute | solution.py:18
  111.7 4.2 %collective-permute-start.11 = (f32[128,16,4]{0,2,1:T(4,128)S(1)}, f32[128,16,4]{0,2,1:T(4,128)S(1)}, u32[]{:S(2)}, u32[]{:S(2)}) collective-permute-start(f32[128,16,4]{0,2,1:T(4,128)S(1)} %get-tuple-element.11), channel_id=1, source_target_pairs={{0,1},{1,2},{2,3},{3,4},{4,5},{5,6},{6,7},{7,8},{8,9},{9,10},{10,1... | collective-permute-start | bytes 98312 | tf_op jit(solution)/shard_map/ppermute | solution.py:18
  114.9 3.3 collective-permute-start.12
  126.5 25.6 %collective-permute-start.13 = (f32[128,8,128]{0,2,1:T(8,128)S(1)}, f32[128,8,128]{0,2,1:T(8,128)S(1)}, u32[]{:S(2)}, u32[]{:S(2)}) collective-permute-start(f32[128,8,128]{0,2,1:T(8,128)S(1)} %fusion.18), channel_id=1, source_target_pairs={{0,128},{128,256},{256,384},{384,512},{512,640},{1,129},{129,257},... | collective-permute-start | bytes 1572872 | tf_op jit(solution)/shard_map/ppermute | solution.py:29
  152.3 16.9 %collective-permute-start.14 = (f32[128,4,128]{0,2,1:T(8,128)S(1)}, f32[128,4,128]{0,2,1:T(8,128)S(1)}, u32[]{:S(2)}, u32[]{:S(2)}) collective-permute-start(f32[128,4,128]{0,2,1:T(8,128)S(1)} %get-tuple-element.19), channel_id=1, source_target_pairs={{0,16},{16,32},{32,48},{48,64},{64,80},{80,96},{96,112},{112,0},{1... | collective-permute-start | bytes 786440 | tf_op jit(solution)/shard_map/ppermute | solution.py:18
  154.2 15.9 %collective-permute-start.15 = (f32[128,4,128]{0,2,1:T(8,128)S(1)}, f32[128,4,128]{0,2,1:T(8,128)S(1)}, u32[]{:S(2)}, u32[]{:S(2)}) collective-permute-start(f32[128,4,128]{0,2,1:T(8,128)S(1)} %get-tuple-element.20), channel_id=1, source_target_pairs={{16,0},{32,16},{48,32},{64,48},{80,64},{96,80},{112,96},{0,112},{1... | collective-permute-start | bytes 786440 | tf_op jit(solution)/shard_map/ppermute | solution.py:21
  170.1 4.5 %collective-permute-start.16 = (f32[128,16,4]{0,2,1:T(4,128)S(1)}, f32[128,16,4]{0,2,1:T(4,128)S(1)}, u32[]{:S(2)}, u32[]{:S(2)}) collective-permute-start(f32[128,16,4]{0,2,1:T(4,128)S(1)} %get-tuple-element.9), channel_id=1, source_target_pairs={{0,1},{1,2},{2,3},{3,4},{4,5},{5,6},{6,7},{7,8},{8,9},{9,10},{10,1... | collective-permute-start | bytes 98312 | tf_op jit(solution)/shard_map/ppermute | solution.py:18
  173.6 3.3 collective-permute-start.17
  185.2 26.0 %collective-permute-start.18 = (f32[128,8,128]{0,2,1:T(8,128)S(1)}, f32[128,8,128]{0,2,1:T(8,128)S(1)}, u32[]{:S(2)}, u32[]{:S(2)}) collective-permute-start(f32[128,8,128]{0,2,1:T(8,128)S(1)} %fusion.17), channel_id=1, source_target_pairs={{0,128},{128,256},{256,384},{384,512},{512,640},{1,129},{129,257},... | collective-permute-start | bytes 1572872 | tf_op jit(solution)/shard_map/ppermute | solution.py:29
  211.4 18.6 %collective-permute-start.19 = (f32[128,4,128]{0,2,1:T(8,128)S(1)}, f32[128,4,128]{0,2,1:T(8,128)S(1)}, u32[]{:S(2)}, u32[]{:S(2)}) collective-permute-start(f32[128,4,128]{0,2,1:T(8,128)S(1)} %get-tuple-element.17), channel_id=1, source_target_pairs={{0,16},{16,32},{32,48},{48,64},{64,80},{80,96},{96,112},{112,0},{1... | collective-permute-start | bytes 786440 | tf_op jit(solution)/shard_map/ppermute | solution.py:18
  213.3 17.6 %collective-permute-start.20 = (f32[128,4,128]{0,2,1:T(8,128)S(1)}, f32[128,4,128]{0,2,1:T(8,128)S(1)}, u32[]{:S(2)}, u32[]{:S(2)}) collective-permute-start(f32[128,4,128]{0,2,1:T(8,128)S(1)} %get-tuple-element.18), channel_id=1, source_target_pairs={{16,0},{32,16},{48,32},{64,48},{80,64},{96,80},{112,96},{0,112},{1... | collective-permute-start | bytes 786440 | tf_op jit(solution)/shard_map/ppermute | solution.py:21
  230.9 2.8 collective-permute-start.21
  230.9 3.4 collective-permute-start.22
  242.6 25.6 %collective-permute-start.23 = (f32[128,8,128]{0,2,1:T(8,128)S(1)}, f32[128,8,128]{0,2,1:T(8,128)S(1)}, u32[]{:S(2)}, u32[]{:S(2)}) collective-permute-start(f32[128,8,128]{0,2,1:T(8,128)S(1)} %fusion.16), channel_id=1, source_target_pairs={{0,128},{128,256},{256,384},{384,512},{512,640},{1,129},{129,257},... | collective-permute-start | bytes 1572872 | tf_op jit(solution)/shard_map/ppermute | solution.py:29
  268.3 16.9 %collective-permute-start.24 = (f32[128,4,128]{0,2,1:T(8,128)S(1)}, f32[128,4,128]{0,2,1:T(8,128)S(1)}, u32[]{:S(2)}, u32[]{:S(2)}) collective-permute-start(f32[128,4,128]{0,2,1:T(8,128)S(1)} %get-tuple-element.15), channel_id=1, source_target_pairs={{0,16},{16,32},{32,48},{48,64},{64,80},{80,96},{96,112},{112,0},{1... | collective-permute-start | bytes 786440 | tf_op jit(solution)/shard_map/ppermute | solution.py:18
  270.3 16.2 %collective-permute-start.25 = (f32[128,4,128]{0,2,1:T(8,128)S(1)}, f32[128,4,128]{0,2,1:T(8,128)S(1)}, u32[]{:S(2)}, u32[]{:S(2)}) collective-permute-start(f32[128,4,128]{0,2,1:T(8,128)S(1)} %get-tuple-element.16), channel_id=1, source_target_pairs={{16,0},{32,16},{48,32},{64,48},{80,64},{96,80},{112,96},{0,112},{1... | collective-permute-start | bytes 786440 | tf_op jit(solution)/shard_map/ppermute | solution.py:21
  286.5 10.0 %collective-permute-start.26 = (f32[128,16,4]{0,2,1:T(4,128)S(1)}, f32[128,16,4]{0,2,1:T(4,128)S(1)}, u32[]{:S(2)}, u32[]{:S(2)}) collective-permute-start(f32[128,16,4]{0,2,1:T(4,128)S(1)} %get-tuple-element.5), channel_id=1, source_target_pairs={{0,1},{1,2},{2,3},{3,4},{4,5},{5,6},{6,7},{7,8},{8,9},{9,10},{10,1... | collective-permute-start | bytes 98312 | tf_op jit(solution)/shard_map/ppermute | solution.py:18
  295.4 3.3 collective-permute-start.27
  307.1 21.7 %collective-permute-start.28 = (f32[128,8,128]{0,2,1:T(8,128)S(1)}, f32[128,8,128]{0,2,1:T(8,128)S(1)}, u32[]{:S(2)}, u32[]{:S(2)}) collective-permute-start(f32[128,8,128]{0,2,1:T(8,128)S(1)} %fusion.15), channel_id=1, source_target_pairs={{0,128},{128,256},{256,384},{384,512},{512,640},{1,129},{129,257},... | collective-permute-start | bytes 1572872 | tf_op jit(solution)/shard_map/ppermute | solution.py:29
  362.2 38.1 %copy-start.2 = (f32[1,1,128,128]{3,2,1,0:T(8,128)S(1)}, f32[1,1,128,128]{3,2,1,0:T(8,128)}, u32[]{:S(2)}) copy-start(f32[1,1,128,128]{3,2,1,0:T(8,128)} %param.15) | copy-start | bytes 196612
  362.2 38.1 %all-to-all-start = ((f32[128,16,128]{0,2,1:T(8,128)}), f32[128,16,128]{0,2,1:T(8,128)S(1)}, u32[]{:S(2)}, u32[]{:S(2)}) async-start(f32[128,16,128]{0,2,1:T(8,128)} %broadcast_multiply_fusion), calls=%async_computation | async-start | bytes 2097152 | tf_op jit(solution)/shard_map/all_to_all | solution.py:85
  (4 other events, 84.8 us)
where the time goes:
time: 410 us; the launch traced here: 403 us
  starting transfers between devices  202 us (49%)
  waiting for transfers between devices  118 us (29%)
  matrix products  41.9 us (10%)
  local copies, waits for them, and re-layouts  31 us (8%)
  other arithmetic  8.23 us (2%)
    ppermute x12, starting transfers between devices, padded_2(): lax.ppermute(lax.slice_in_dim(block, 0, width, axis=dim), axis, backward)  86.4 us
    ppermute x5, starting transfers between devices, passed_along(): return lax.ppermute(x, axis, pairs)  72.5 us
    ppermute x5, waiting for transfers between devices, passed_along(): return lax.ppermute(x, axis, pairs)  51.7 us
    dot_general x20, matrix products, advance_slot(): jnp.einsum('mn,nlk->mlk', mixing, shifted_state, precision=lax.Precision....  40.9 us
    ppermute x12, starting transfers between devices, padded_2(): lax.ppermute(lax.slice_in_dim(block, block.shape[dim] - width, None, axis...  32.8 us
    all_to_all x1, waiting for transfers between devices, local(): lax.all_to_all(profile, 'obs', split_axis=1, concat_axis=1, tiled=True)  27 us
    ppermute x12, waiting for transfers between devices, padded_2(): lax.ppermute(lax.slice_in_dim(block, block.shape[dim] - width, None, axis...  25.9 us
    gather x3, local copies, waits for them, and re-layouts, local(): profile = profile + weights[corner] * jnp.take(flat, cells[corner], axis=1)  20.7 us
  transfers between devices with their start and end apart: 30, of which 26 were waited for; matrix products, arithmetic and copies ran while one was open for 1% of the time, Pallas kernels for 0%

commit v1 on v0

v1 whole, which is shorter than its diff:
```python
import functools

import jax
import jax.numpy as jnp
from jax import lax
from jax.experimental import pallas as pl
from jax.experimental.pallas import tpu as pltpu
from jax.sharding import Mesh
from jax.sharding import PartitionSpec as P

STEPS = 4
WIDE = 11
WINDOW = WIDE + 2 * STEPS
LANE_B = 32

mixing_rate = 0.15

SMEM = functools.partial(pl.BlockSpec, memory_space=pltpu.SMEM)
VMEM = functools.partial(pl.BlockSpec, memory_space=pltpu.VMEM)


def starts_of(width, planes):
    return [width * j // planes for j in range(planes + 1)]


def halves(x):
    high = x.astype(jnp.bfloat16)
    low = (x - high.astype(jnp.float32)).astype(jnp.bfloat16)
    return high, low


def cut_kernel(planes, odd_ref, forcing_ref, rates_ref, out_ref, turned):
    levels, width_x, width_y = forcing_ref.shape
    odd = odd_ref[0]
    for x in range(width_x):
        turned[:, x, :] = forcing_ref[:, x, :].T
    lane = lax.broadcasted_iota(jnp.int32, (width_x, rates_ref.shape[2]), 1)
    for j, start in enumerate(starts_of(width_y, planes)[:-1]):
        place = jnp.where(odd == 1, planes - 1 - j, j)
        out_ref[place, 0:WIDE] = turned[start : start + WIDE]
        whole = rates_ref.shape[2]
        east = pltpu.roll(rates_ref[0], (whole - start) % whole, 1)
        north = pltpu.roll(rates_ref[1], (whole + LANE_B - start) % whole, 1)
        both = jnp.where(lane < LANE_B, east, north)
        out_ref[place, WIDE] = both[:, :levels]


def spread_kernel(size_ref, first_ref, own_ref, up_ref, down_ref, rates_ref):
    nx, nz, rows, part, _ = first_ref.shape
    size = size_ref[0]
    for z in range(nz):
        for x in range(nx):
            at = (z * nx + x) * part
            own_ref[:, at : at + part, :] = first_ref[x, z, 0:WIDE]
            for s in range(rows - WIDE):
                rates_ref[s, at : at + part, :] = first_ref[x, z, WIDE + s]
    down_ref[...] = own_ref[0:STEPS]
    up_ref[...] = own_ref[pl.ds(size - STEPS, STEPS)]


def round_kernel(
    last, at_slot, size_ref, own_ref, low_ref, high_ref, rates_ref, forcing_ref, mix_ref, *rest
):
    if last:
        part_ref, ping, pong, east_rate, north_rate, table = rest
    else:
        next_ref, up_ref, down_ref, part_ref, ping, pong, east_rate, north_rate, table = rest
    size = size_ref[0]
    x_place = size_ref[1]
    whole_x = own_ref.shape[1]
    levels = own_ref.shape[2]
    ping[0:STEPS] = low_ref[...]
    ping[STEPS : STEPS + WIDE] = own_ref[...]
    ping[WINDOW - 1] = jnp.zeros((whole_x, levels), jnp.float32)
    ping[pl.ds(STEPS + size, STEPS)] = high_ref[...]
    for y in range(1, WINDOW - 1):
        east_rate[y] = jnp.broadcast_to(rates_ref[:, y : y + 1], (whole_x, levels))
        north_rate[y] = jnp.broadcast_to(
            rates_ref[:, LANE_B + y : LANE_B + y + 1], (whole_x, levels)
        )
    mix_high, mix_low = halves(mix_ref[...])
    table[0:levels, 0:levels] = mix_high
    table[levels:, 0:levels] = mix_high
    table[0:levels, levels:] = mix_low
    table[levels:, levels:] = mix_low
    bufs = (ping, pong)
    for step in range(STEPS):
        source, target = bufs[step % 2], bufs[(step + 1) % 2]
        first, end = step + 1, WINDOW - 1 - step
        pieces = []
        for y in range(first, end):
            centre = source[y]
            northern = source[y + 1]
            southern = source[y - 1]
            eastern = pltpu.roll(centre, whole_x - 1, 0)
            western = pltpu.roll(centre, 1, 0)
            z = centre + east_rate[y] * (eastern - western) + north_rate[y] * (northern - southern)
            z = z + mixing_rate * (
                (eastern + western) + (northern + southern) - 4.0 * centre
            )
            target[y] = z
        count = end - first
        z = target[first:end].reshape(count * whole_x, levels)
        high, low = halves(z)
        both = jnp.dot(
            jnp.concatenate([high, low], axis=1), table[...], preferred_element_type=jnp.float32
        )
        z = z + (both[:, :levels] + both[:, levels:])
        target[first:end] = z.reshape(count, whole_x, levels)
    result = bufs[STEPS % 2]
    nz, _, part, _ = part_ref.shape
    for z in range(nz):
        at = pl.multiple_of(z * (whole_x // nz) + x_place * part, part)
        part_ref[z] = result[STEPS : STEPS + WIDE, pl.ds(at, part), :]
    if not last:
        nx = forcing_ref.shape[0]
        for z in range(nz):
            for x in range(nx):
                at = (z * nx + x) * part
                next_ref[:, at : at + part, :] = (
                    result[STEPS : STEPS + WIDE, at : at + part, :] + forcing_ref[x, z, at_slot]
                )
        down_ref[...] = next_ref[0:STEPS]
        up_ref[...] = next_ref[pl.ds(size - STEPS, STEPS)]


def observe_kernel(
    planes, odd_ref, strips_ref, forcing_ref, cells_ref, weights_ref, state_ref, out_ref,
    turned, split,
):
    levels, width_x, width_y = forcing_ref.shape

    @pl.when(pl.program_id(0) == 0)
    def _():
        odd = odd_ref[0]
        starts = starts_of(width_y, planes)
        for j in range(planes):
            place = jnp.where(odd == 1, planes - 1 - j, j)
            turned[starts[j] : starts[j] + WIDE] = strips_ref[place]
        for x in range(width_x):
            value = turned[:, x, :].T + forcing_ref[:, x, :]
            state_ref[:, x, :] = value
            high, low = halves(value)
            split[0:levels, x * width_y : (x + 1) * width_y] = high
            split[levels:, x * width_y : (x + 1) * width_y] = low

    columns = width_x * width_y
    capacity = cells_ref.shape[1]
    column = lax.broadcasted_iota(jnp.int32, (columns, capacity), 0)
    table = jnp.zeros((columns, capacity), jnp.float32)
    for corner in range(cells_ref.shape[0]):
        cell = cells_ref[corner : corner + 1, :]
        weight = weights_ref[corner : corner + 1, :]
        table = table + jnp.where(column == cell, weight, 0.0)
    high, low = halves(table)
    both = jnp.dot(
        split[...], jnp.concatenate([high, low], axis=1), preferred_element_type=jnp.float32
    )
    out_ref[0] = both[:levels, :capacity] + (both[:levels, capacity:] + both[levels:, :capacity])


def channel_kernel(table_ref, profile_ref, out_ref):
    table_high, table_low = halves(table_ref[...])
    left = jnp.concatenate([table_high, table_low, table_high], axis=1)
    blocks, _, capacity = profile_ref.shape
    for block in range(blocks):
        high, low = halves(profile_ref[block])
        right = jnp.concatenate([high, high, low], axis=0)
        out_ref[:, block * capacity : (block + 1) * capacity] = jnp.dot(
            left, right, preferred_element_type=jnp.float32
        )


def f32(*shape):
    return jax.ShapeDtypeStruct(shape, jnp.float32)


def local(forcing, winds, mixing, observation_columns, obs_weights, obs_counts, jacobian):
    slots = lax.axis_size("slot")
    halves_z = lax.axis_size("zhi")
    parts_x = lax.axis_size("x")
    owners = lax.axis_size("obs")
    planes = slots * halves_z
    rounds = slots - 1
    block = forcing[0]
    levels, width_x, width_y = block.shape
    whole_x = width_x * parts_x * halves_z
    starts = starts_of(width_y, planes)

    place_o = lax.axis_index("obs")
    place_z = lax.axis_index("zhi") * slots + lax.axis_index("slot")
    odd = (place_o % 2).astype(jnp.int32)
    strip = jnp.where(odd == 1, planes - 1 - place_z, place_z)
    size = (width_y * (strip + 1)) // planes - (width_y * strip) // planes
    odd = odd.reshape(1)
    sizes = jnp.stack([size.astype(jnp.int32), lax.axis_index("x").astype(jnp.int32)])

    order = []
    for o in range(owners):
        along = range(planes) if o % 2 == 0 else range(planes - 1, -1, -1)
        order += [((z % slots) * halves_z + z // slots) * owners + o for z in along]
    upward = [(order[i - 1], order[i]) for i in range(len(order))]
    downward = [(target, source) for source, target in upward]
    chain = ("slot", "zhi", "obs")

    rates = winds[:, 0]
    ring = [(i, (i + 1) % owners) for i in range(owners)]
    back = [(target, source) for source, target in ring]
    rates_low = lax.ppermute(rates[:, :, width_y - STEPS :], "obs", ring)
    rates_high = lax.ppermute(rates[:, :, :STEPS], "obs", back)
    rates = jnp.concatenate(
        [rates_low, rates, rates_high, jnp.zeros((2, width_x, width_y - 2 * STEPS), jnp.float32)],
        axis=2,
    )

    cut = pl.pallas_call(
        functools.partial(cut_kernel, planes),
        out_shape=f32(planes, WIDE + 1, width_x, levels),
        in_specs=[SMEM(), VMEM(), VMEM()],
        out_specs=VMEM(),
        scratch_shapes=[pltpu.VMEM((width_y, width_x, levels), jnp.float32)],
        cost_estimate=pl.CostEstimate(flops=4000000, bytes_accessed=1100000, transcendentals=0),
        name="cut",
    )(odd, block, rates)
    strips = lax.all_to_all(cut, ("zhi", "slot"), 0, 0, tiled=True)
    strips = strips.reshape(halves_z, slots, WIDE + 1, width_x, levels)
    first = jnp.concatenate(
        [strips[:, 0, :WIDE], strips[:, :rounds, WIDE]], axis=1
    )
    later = strips[:, 1:rounds, :WIDE]
    first = lax.all_to_all(
        jnp.broadcast_to(first, (parts_x,) + first.shape), "x", 0, 0, tiled=True
    ).reshape((parts_x,) + first.shape)
    later = lax.all_to_all(
        jnp.broadcast_to(later, (parts_x,) + later.shape), "x", 0, 0, tiled=True
    ).reshape((parts_x,) + later.shape)

    strip_shape = f32(WIDE, whole_x, levels)
    edge_shape = f32(STEPS, whole_x, levels)
    part_shape = f32(halves_z, WIDE, width_x, levels)
    own, up, down, rates = pl.pallas_call(
        spread_kernel,
        out_shape=(strip_shape, edge_shape, edge_shape, f32(rounds, whole_x, levels)),
        in_specs=[SMEM(), VMEM()],
        out_specs=(VMEM(),) * 4,
        cost_estimate=pl.CostEstimate(flops=1000000, bytes_accessed=1500000, transcendentals=0),
        name="spread",
    )(sizes, first)

    turned_mixing = mixing.T
    window = pltpu.VMEM((WINDOW, whole_x, levels), jnp.float32)
    kept = []
    for index in range(rounds):
        last = index == rounds - 1
        low = lax.ppermute(up, chain, upward)
        high = lax.ppermute(down, chain, downward)
        shapes = (part_shape,) if last else (strip_shape, edge_shape, edge_shape, part_shape)
        results = pl.pallas_call(
            functools.partial(round_kernel, last, min(index, rounds - 2)),
            out_shape=shapes,
            in_specs=[SMEM()] + [VMEM()] * 6,
            out_specs=(VMEM(),) * len(shapes),
            scratch_shapes=[window] * 4 + [pltpu.VMEM((2 * levels, 2 * levels), jnp.bfloat16)],
            cost_estimate=pl.CostEstimate(
                flops=400000000, bytes_accessed=3000000, transcendentals=0
            ),
            name="round",
        )(sizes, own, low, high, rates[index], later, turned_mixing)
        kept.append(results[-1])
        if not last:
            own, up, down = results[:3]

    home = jnp.stack([jnp.zeros_like(kept[0])] + kept, axis=1)
    home = home.reshape(planes, WIDE, width_x, levels)
    home = lax.all_to_all(home, ("zhi", "slot"), 0, 0, tiled=True)

    cells = observation_columns[:, 0]
    weights = obs_weights[:, 0]
    points, row_count = cells.shape
    capacity = row_count // owners
    live = lax.broadcasted_iota(jnp.int32, (owners, capacity), 1) < obs_counts[0, 0][:, None]
    weights = jnp.where(live.reshape(1, row_count), weights, 0.0)

    columns = width_x * width_y
    state, profile = pl.pallas_call(
        functools.partial(observe_kernel, planes),
        out_shape=(f32(levels, width_x, width_y), f32(owners, levels, capacity)),
        grid=(owners,),
        in_specs=[
            SMEM(),
            pl.BlockSpec((planes, WIDE, width_x, levels), lambda q: (0, 0, 0, 0)),
            pl.BlockSpec((levels, width_x, width_y), lambda q: (0, 0, 0)),
            pl.BlockSpec((points, capacity), lambda q: (0, q)),
            pl.BlockSpec((points, capacity), lambda q: (0, q)),
        ],
        out_specs=(
            pl.BlockSpec((levels, width_x, width_y), lambda q: (0, 0, 0)),
            pl.BlockSpec((1, levels, capacity), lambda q: (q, 0, 0)),
        ),
        scratch_shapes=[
            pltpu.VMEM((width_y, width_x, levels), jnp.float32),
            pltpu.VMEM((2 * levels, columns), jnp.bfloat16),
        ],
        cost_estimate=pl.CostEstimate(
            flops=2000000000, bytes_accessed=3000000, transcendentals=0
        ),
        name="observe",
    )(odd, home, block, cells, weights)

    profile = lax.all_to_all(profile, "obs", 0, 0, tiled=True)
    channels = jacobian.shape[2]
    group = 4
    radiance = pl.pallas_call(
        channel_kernel,
        out_shape=f32(channels, row_count),
        grid=(owners // group,),
        in_specs=[
            pl.BlockSpec((channels, levels), lambda q: (0, 0)),
            pl.BlockSpec((group, levels, capacity), lambda q: (q, 0, 0)),
        ],
        out_specs=pl.BlockSpec((channels, group * capacity), lambda q: (0, q)),
        cost_estimate=pl.CostEstimate(
            flops=200000000, bytes_accessed=2200000, transcendentals=0
        ),
        name="channel",
    )(jacobian[0, 0], profile)
    return (state[None], radiance[None])


def solution(mesh):
    slots, tiles, owners = (mesh.shape[name] for name in ("slot", "tile", "obs"))
    fine = Mesh(
        mesh.devices.reshape(slots, 2, tiles // 2, owners), ("slot", "zhi", "x", "obs")
    )
    tile = ("zhi", "x")
    return jax.shard_map(
        local,
        mesh=fine,
        in_specs=(
            P("slot", None, tile, "obs"),
            P(None, "slot", tile, "obs"),
            P(),
            P(None, "slot", tile + ("obs",)),
            P(None, "slot", tile + ("obs",)),
            P("slot", tile + ("obs",), None),
            P("slot", "obs", None, None),
        ),
        out_specs=(P("slot", None, tile, "obs"), P("slot", None, tile + ("obs",))),
        check_vma=False,
    )
```

time: 410 us -> 241 us (0.59); the launches traced: 403 us -> 239 us
  starting transfers between devices: 202 us -> 58.5 us
  blocking collectives: 0 us -> 75.8 us
  waiting for transfers between devices: 118 us -> 45 us
  matrix products: 41.9 us -> 0 us
  Pallas kernels: 0 us -> 40.4 us
  local copies, waits for them, and re-layouts: 31 us -> 15.9 us
  other arithmetic: 8.23 us -> 2.73 us
    ppermute x29 -> x12, starting transfers between devices: 192 us -> 47.2 us  [the longest x5 25.6 us: local(): low = lax.ppermute(up, chain, upward)]
    all_to_all x0 -> x2, blocking collectives: none -> 75.8 us  [the longest x1 41.2 us: local(): profile = lax.all_to_all(profile, 'obs', 0, 0, tiled=True)]
    ppermute x29 -> x12, waiting for transfers between devices: 91.4 us -> 17.7 us  [the longest x5 16.9 us: local(): high = lax.ppermute(down, chain, downward)]
    dot_general x21 -> x0, matrix products: 41.9 us -> none  [the longest x20 40.9 us: advance_slot(): jnp.einsum('mn,nlk->mlk', mixing, shifted_state, precision=lax.Precision....]
    pallas_call x0 -> x9, Pallas kernels: none -> 40.4 us  [the longest x5 20 us: local(): pl.pallas_call(functools.partial(round_kernel, last, min(index, rounds -...]
    gather x4 -> x0, local copies, waits for them, and re-layouts: 26.2 us -> none  [the longest x3 20.7 us: local(): profile = profile + weights[corner] * jnp.take(flat, cells[corner], axis=1)]
    add x6 -> x0, other arithmetic: 6.18 us -> none  [the longest x1 5.77 us: local(): profile = profile + weights[corner] * jnp.take(flat, cells[corner], axis=1)]
    unnamed x15 -> x41, local copies, waits for them, and re-layouts: 3.58 us -> 9.56 us
  transfers between devices with their start and end apart: 30 -> 15, of which waited for: 26 -> 9; matrix products, arithmetic and copies ran while one was open for 1% -> 3% of each run, Pallas kernels for 0% -> 1%
where the time goes in v1:
time: 241 us; the launch traced here: 239 us
  blocking collectives  75.8 us (31%)
  starting transfers between devices  58.5 us (24%)
  waiting for transfers between devices  45 us (19%)
  Pallas kernels  40.4 us (17%)
  local copies, waits for them, and re-layouts  15.9 us (7%)
  other arithmetic  2.73 us (1%)
    all_to_all x1, blocking collectives, local(): profile = lax.all_to_all(profile, 'obs', 0, 0, tiled=True)  41.2 us
    all_to_all x1, blocking collectives, local(): strips = lax.all_to_all(cut, ('zhi', 'slot'), 0, 0, tiled=True)  34.5 us
    ppermute x5, starting transfers between devices, local(): low = lax.ppermute(up, chain, upward)  25.6 us
    all_to_all x1, waiting for transfers between devices, local(): home = lax.all_to_all(home, ('zhi', 'slot'), 0, 0, tiled=True)  20.4 us
    pallas_call x5, Pallas kernels, local(): pl.pallas_call(functools.partial(round_kernel, last, min(index, rounds -...  20 us
    ppermute x5, waiting for transfers between devices, local(): high = lax.ppermute(down, chain, downward)  16.9 us
    pallas_call x1, Pallas kernels, local(): pl.pallas_call(functools.partial(observe_kernel, planes), out_shape=(f32(...  12.1 us
    ppermute x5, starting transfers between devices, local(): high = lax.ppermute(down, chain, downward)  11.1 us
  transfers between devices with their start and end apart: 15, of which 9 were waited for; matrix products, arithmetic and copies ran while one was open for 3% of the time, Pallas kernels for 1%

profile of v1, /device:TPU:1, one launch (start us, length us, event | category | flops | bytes accessed | tf_op | source)
XLA Modules:
  0.0 239.2 jit_solution(674589279587247949)
XLA Ops:
  1.5 2.7 %collective-permute-start = (f32[2,8,4]{2,1,0:T(8,128)S(1)}, f32[2,8,4]{2,1,0:T(8,128)S(1)}, u32[]{:S(2)}, u32[]{:S(2)}) collective-permute-start(f32[2,8,4]{2,1,0:T(8,128)S(1)} %get-tuple-element.51), channel_id=1, source_target_pairs={{0,1},{1,2},{2,3},{3,4},{4,5},{5,6},{6,7},{7,8},{8,9},{9,10},{10,1... | collective-permute-start | bytes 776 | tf_op jit(solution)/shard_map/ppermute | solution.py:209
  4.2 7.8 %collective-permute-start.1 = (f32[2,8,4]{2,1,0:T(8,128)S(1)}, f32[2,8,4]{2,1,0:T(8,128)S(1)}, u32[]{:S(2)}, u32[]{:S(2)}) collective-permute-start(f32[2,8,4]{2,1,0:T(8,128)S(1)} %get-tuple-element.52), channel_id=1, source_target_pairs={{1,0},{2,1},{3,2},{4,3},{5,4},{6,5},{7,6},{8,7},{9,8},{10,9},{11,1... | collective-permute-start | bytes 776 | tf_op jit(solution)/shard_map/ppermute | solution.py:210
  14.2 2.5 %cut.1 = f32[12,12,8,128]{3,2,1,0:T(8,128)} custom-call(s32[1]{0:T(128)} %bitcast.odd_ref, f32[128,8,128]{2,1,0:T(8,128)} %bitcast.52, f32[2,8,256]{2,1,0:T(8,128)} %maximum_maximum_fusion.rates_ref), custom_call_target="tpu_custom_call" | custom-call | flops 4000000 | bytes 1100000 | tf_op jit(solution)/shard_map/cut/pallas_call | solution.py:216
  16.7 34.5 %all_to_all.25 = f32[12,12,8,128]{3,2,1,0:T(8,128)S(1)} all-to-all(f32[12,12,8,128]{3,2,1,0:T(8,128)} %cut.1), channel_id=1, replica_groups=mesh['slot'=6,'zhi'=2,'x'=4,'obs'=16] {'zhi','slot'}, dimensions={0} | all-to-all | bytes 1179648 | tf_op jit(solution)/shard_map/all_to_all | solution.py:225
  52.1 4.0 %all-to-all-start.1 = ((f32[4,2,16,8,128]{4,3,2,1,0:T(8,128)}), f32[4,2,16,8,128]{4,3,2,1,0:T(8,128)S(1)}, u32[]{:S(2)}, u32[]{:S(2)}) async-start(f32[4,2,16,8,128]{4,3,2,1,0:T(8,128)} %broadcast_in_dim.28), calls=%async_computation.1 | async-start | bytes 1048576 | tf_op jit(solution)/shard_map/all_to_all | solution.py:231
  56.1 6.9 %all-to-all-done.1.first_ref = f32[4,2,16,8,128]{4,3,2,1,0:T(8,128)S(1)} async-done(((f32[4,2,16,8,128]{4,3,2,1,0:T(8,128)}), f32[4,2,16,8,128]{4,3,2,1,0:T(8,128)S(1)}, u32[]{:S(2)}, u32[]{:S(2)}) %all-to-all-start.1) | async-done | bytes 524320 | tf_op jit(solution)/shard_map/all_to_all | solution.py:231
  64.3 3.7 %all-to-all-start.2 = ((f32[4,2,4,11,8,128]{5,4,3,2,1,0:T(8,128)}), f32[4,2,4,11,8,128]{5,4,3,2,1,0:T(8,128)S(1)}, u32[]{:S(2)}, u32[]{:S(2)}) async-start(f32[4,2,4,11,8,128]{5,4,3,2,1,0:T(8,128)} %broadcast_in_dim.29), calls=%async_computation.2 | async-start | bytes 2883584 | tf_op jit(solution)/shard_map/all_to_all | solution.py:234
  69.5 2.0 spread.1
  71.5 7.8 %collective-permute-start.2 = (f32[4,64,128]{2,1,0:T(8,128)}, f32[4,64,128]{2,1,0:T(8,128)S(1)}, u32[]{:S(2)}, u32[]{:S(2)}) collective-permute-start(f32[4,64,128]{2,1,0:T(8,128)} %get-tuple-element.25), channel_id=1, source_target_pairs={{15,0},{0,128},{128,256},{256,384},{384,512},{512,640},{640,64},{6... | collective-permute-start | bytes 393224 | tf_op jit(solution)/shard_map/ppermute | solution.py:255
  79.3 1.9 collective-permute-start.3
  82.7 3.4 %collective-permute-done.3.high_ref = f32[4,64,128]{2,1,0:T(8,128)S(1)} collective-permute-done((f32[4,64,128]{2,1,0:T(8,128)}, f32[4,64,128]{2,1,0:T(8,128)S(1)}, u32[]{:S(2)}, u32[]{:S(2)}) %collective-permute-start.3) | collective-permute-done | bytes 131104 | tf_op jit(solution)/shard_map/ppermute | solution.py:256
  87.3 4.0 %round.5 = (f32[11,64,128]{2,1,0:T(8,128)}, f32[4,64,128]{2,1,0:T(8,128)}, f32[4,64,128]{2,1,0:T(8,128)}, f32[2,11,8,128]{3,2,1,0:T(8,128)}) custom-call(s32[2]{0:T(128)} %pad_add_fusion.size_ref, f32[11,64,128]{2,1,0:T(8,128)} %get-tuple-element.24.own_ref, f32[4,64,128]{2,1,0:T(8,128)} %copy-done.3, f32[4,64,128]{2,1,0:T(8,128)} %copy-done.4, ...), custom_call_target="tpu_custom_call" | custom-call | flops 400000000 | bytes 3000000 | tf_op jit(solution)/shard_map/round/pallas_call | solution.py:258
  91.3 9.1 %collective-permute-start.4 = (f32[4,64,128]{2,1,0:T(8,128)}, f32[4,64,128]{2,1,0:T(8,128)S(1)}, u32[]{:S(2)}, u32[]{:S(2)}) collective-permute-start(f32[4,64,128]{2,1,0:T(8,128)} %get-tuple-element.30), channel_id=1, source_target_pairs={{15,0},{0,128},{128,256},{256,384},{384,512},{512,640},{640,64},{6... | collective-permute-start | bytes 393224 | tf_op jit(solution)/shard_map/ppermute | solution.py:255
  100.4 1.9 collective-permute-start.5
  103.2 3.7 %collective-permute-done.5.high_ref = f32[4,64,128]{2,1,0:T(8,128)S(1)} collective-permute-done((f32[4,64,128]{2,1,0:T(8,128)}, f32[4,64,128]{2,1,0:T(8,128)S(1)}, u32[]{:S(2)}, u32[]{:S(2)}) %collective-permute-start.5) | collective-permute-done | bytes 131104 | tf_op jit(solution)/shard_map/ppermute | solution.py:256
  107.6 4.0 %round.6 = (f32[11,64,128]{2,1,0:T(8,128)}, f32[4,64,128]{2,1,0:T(8,128)}, f32[4,64,128]{2,1,0:T(8,128)}, f32[2,11,8,128]{3,2,1,0:T(8,128)}) custom-call(s32[2]{0:T(128)} %pad_add_fusion.size_ref, f32[11,64,128]{2,1,0:T(8,128)} %get-tuple-element.29.own_ref, f32[4,64,128]{2,1,0:T(8,128)} %copy-done.5, f32[4,64,128]{2,1,0:T(8,128)} %copy-done.9, ...), custom_call_target="tpu_custom_call" | custom-call | flops 400000000 | bytes 3000000 | tf_op jit(solution)/shard_map/round/pallas_call | solution.py:258
  111.6 3.5 %collective-permute-start.6 = (f32[4,64,128]{2,1,0:T(8,128)}, f32[4,64,128]{2,1,0:T(8,128)S(1)}, u32[]{:S(2)}, u32[]{:S(2)}) collective-permute-start(f32[4,64,128]{2,1,0:T(8,128)} %get-tuple-element.34), channel_id=1, source_target_pairs={{15,0},{0,128},{128,256},{256,384},{384,512},{512,640},{640,64},{6... | collective-permute-start | bytes 393224 | tf_op jit(solution)/shard_map/ppermute | solution.py:255
  118.0 3.7 %collective-permute-done.7.high_ref = f32[4,64,128]{2,1,0:T(8,128)S(1)} collective-permute-done((f32[4,64,128]{2,1,0:T(8,128)}, f32[4,64,128]{2,1,0:T(8,128)S(1)}, u32[]{:S(2)}, u32[]{:S(2)}) %collective-permute-start.7) | collective-permute-done | bytes 131104 | tf_op jit(solution)/shard_map/ppermute | solution.py:256
  122.3 4.0 %round.7 = (f32[11,64,128]{2,1,0:T(8,128)}, f32[4,64,128]{2,1,0:T(8,128)}, f32[4,64,128]{2,1,0:T(8,128)}, f32[2,11,8,128]{3,2,1,0:T(8,128)}) custom-call(s32[2]{0:T(128)} %pad_add_fusion.size_ref, f32[11,64,128]{2,1,0:T(8,128)} %get-tuple-element.33.own_ref, f32[4,64,128]{2,1,0:T(8,128)} %copy-done.6, f32[4,64,128]{2,1,0:T(8,128)} %copy-done.10, ...), custom_call_target="tpu_custom_call" | custom-call | flops 400000000 | bytes 3000000 | tf_op jit(solution)/shard_map/round/pallas_call | solution.py:258
  126.3 2.5 %collective-permute-start.8 = (f32[4,64,128]{2,1,0:T(8,128)}, f32[4,64,128]{2,1,0:T(8,128)S(1)}, u32[]{:S(2)}, u32[]{:S(2)}) collective-permute-start(f32[4,64,128]{2,1,0:T(8,128)} %get-tuple-element.38), channel_id=1, source_target_pairs={{15,0},{0,128},{128,256},{256,384},{384,512},{512,640},{640,64},{6... | collective-permute-start | bytes 393224 | tf_op jit(solution)/shard_map/ppermute | solution.py:255
  128.8 2.8 %collective-permute-start.9 = (f32[4,64,128]{2,1,0:T(8,128)}, f32[4,64,128]{2,1,0:T(8,128)S(1)}, u32[]{:S(2)}, u32[]{:S(2)}) collective-permute-start(f32[4,64,128]{2,1,0:T(8,128)} %get-tuple-element.39), channel_id=1, source_target_pairs={{0,15},{128,0},{256,128},{384,256},{512,384},{640,512},{64,640},{1... | collective-permute-start | bytes 393224 | tf_op jit(solution)/shard_map/ppermute | solution.py:256
  132.5 2.8 %collective-permute-done.9.high_ref = f32[4,64,128]{2,1,0:T(8,128)S(1)} collective-permute-done((f32[4,64,128]{2,1,0:T(8,128)}, f32[4,64,128]{2,1,0:T(8,128)S(1)}, u32[]{:S(2)}, u32[]{:S(2)}) %collective-permute-start.9) | collective-permute-done | bytes 131104 | tf_op jit(solution)/shard_map/ppermute | solution.py:256
  135.9 4.0 %round.8 = (f32[11,64,128]{2,1,0:T(8,128)}, f32[4,64,128]{2,1,0:T(8,128)}, f32[4,64,128]{2,1,0:T(8,128)}, f32[2,11,8,128]{3,2,1,0:T(8,128)}) custom-call(s32[2]{0:T(128)} %pad_add_fusion.size_ref, f32[11,64,128]{2,1,0:T(8,128)} %get-tuple-element.37.own_ref, f32[4,64,128]{2,1,0:T(8,128)} %copy-done.7, f32[4,64,128]{2,1,0:T(8,128)} %copy-done.11, ...), custom_call_target="tpu_custom_call" | custom-call | flops 400000000 | bytes 3000000 | tf_op jit(solution)/shard_map/round/pallas_call | solution.py:258
  140.0 2.7 %collective-permute-start.10 = (f32[4,64,128]{2,1,0:T(8,128)}, f32[4,64,128]{2,1,0:T(8,128)S(1)}, u32[]{:S(2)}, u32[]{:S(2)}) collective-permute-start(f32[4,64,128]{2,1,0:T(8,128)} %get-tuple-element.42), channel_id=1, source_target_pairs={{15,0},{0,128},{128,256},{256,384},{384,512},{512,640},{640,64},{6... | collective-permute-start | bytes 393224 | tf_op jit(solution)/shard_map/ppermute | solution.py:255
  142.7 2.6 %collective-permute-start.11 = (f32[4,64,128]{2,1,0:T(8,128)}, f32[4,64,128]{2,1,0:T(8,128)S(1)}, u32[]{:S(2)}, u32[]{:S(2)}) collective-permute-start(f32[4,64,128]{2,1,0:T(8,128)} %get-tuple-element.43), channel_id=1, source_target_pairs={{0,15},{128,0},{256,128},{384,256},{512,384},{640,512},{64,640},{1... | collective-permute-start | bytes 393224 | tf_op jit(solution)/shard_map/ppermute | solution.py:256
  146.2 3.5 %collective-permute-done.11.high_ref = f32[4,64,128]{2,1,0:T(8,128)S(1)} collective-permute-done((f32[4,64,128]{2,1,0:T(8,128)}, f32[4,64,128]{2,1,0:T(8,128)S(1)}, u32[]{:S(2)}, u32[]{:S(2)}) %collective-permute-start.11) | collective-permute-done | bytes 131104 | tf_op jit(solution)/shard_map/ppermute | solution.py:256
  150.3 3.8 %round.9 = f32[2,11,8,128]{3,2,1,0:T(8,128)} custom-call(s32[2]{0:T(128)} %pad_add_fusion.size_ref, f32[11,64,128]{2,1,0:T(8,128)} %get-tuple-element.41.own_ref, f32[4,64,128]{2,1,0:T(8,128)} %copy-done.8, f32[4,64,128]{2,1,0:T(8,128)} %copy-done.12, f32[64,128]{1,0:T(8,128)} %get-tuple-element.46.rates_ref, f32[4,2,4,11,8,128]{5,4,3,2,1,0:T(8,128)} %copy-done, ...), custom_call_target="tpu_custom_call" | custom-call | flops 400000000 | bytes 3000000 | tf_op jit(solution)/shard_map/round/pallas_call | solution.py:258
  155.9 3.6 %all-to-all-start.3 = ((f32[12,11,8,128]{3,2,1,0:T(8,128)}), f32[12,11,8,128]{3,2,1,0:T(8,128)S(1)}, u32[]{:S(2)}, u32[]{:S(2)}) async-start(f32[12,11,8,128]{3,2,1,0:T(8,128)} %bitcast.19), calls=%async_computation.3 | async-start | bytes 1081344 | tf_op jit(solution)/shard_map/all_to_all | solution.py:275
  160.8 20.4 %all-to-all-done.3.strips_ref = f32[12,11,8,128]{3,2,1,0:T(8,128)S(1)} async-done(((f32[12,11,8,128]{3,2,1,0:T(8,128)}), f32[12,11,8,128]{3,2,1,0:T(8,128)S(1)}, u32[]{:S(2)}, u32[]{:S(2)}) %all-to-all-start.3) | async-done | bytes 540704 | tf_op jit(solution)/shard_map/all_to_all | solution.py:275
  182.0 12.1 %observe.1 = (f32[128,8,128]{2,1,0:T(8,128)}, f32[16,128,128]{2,1,0:T(8,128)}) custom-call(s32[1]{0:T(128)} %bitcast.odd_ref, f32[12,11,8,128]{3,2,1,0:T(8,128)} %copy-done.2, f32[128,8,128]{2,1,0:T(8,128)} %bitcast.53, s32[4,2048]{1,0:T(4,128)} %bitcast.57, f32[4,2048]{1,0:T(4,128)} %bitcast_select_fusion.weights_ref), custom_call_target="tpu_custom_call" | custom-call | flops 2000000000 | bytes 3000000 | tf_op jit(solution)/shard_map/observe/pallas_call | solution.py:285
  194.1 41.2 %all_to_all.26.profile_ref = f32[16,128,128]{2,1,0:T(8,128)} all-to-all(f32[16,128,128]{2,1,0:T(8,128)} %get-tuple-element.45), channel_id=1, replica_groups=mesh['slot'=6,'zhi'=2,'x'=4,'obs'=16] {'obs'}, dimensions={0} | all-to-all | bytes 2097152 | tf_op jit(solution)/shard_map/all_to_all | solution.py:310
  235.3 3.9 %channel.1 = f32[128,2048]{1,0:T(8,128)} custom-call(f32[128,128]{1,0:T(8,128)} %bitcast.56, f32[16,128,128]{2,1,0:T(8,128)} %all_to_all.26.profile_ref), custom_call_target="tpu_custom_call" | custom-call | flops 200000000 | bytes 2200000 | tf_op jit(solution)/shard_map/channel/pallas_call | solution.py:313
  (66 shorter events, 21.4 us)
Async XLA Ops:
  1.5 11.1 %collective-permute-start = (f32[2,8,4]{2,1,0:T(8,128)S(1)}, f32[2,8,4]{2,1,0:T(8,128)S(1)}, u32[]{:S(2)}, u32[]{:S(2)}) collective-permute-start(f32[2,8,4]{2,1,0:T(8,128)S(1)} %get-tuple-element.51), channel_id=1, source_target_pairs={{0,1},{1,2},{2,3},{3,4},{4,5},{5,6},{6,7},{7,8},{8,9},{9,10},{10,1... | collective-permute-start | bytes 776 | tf_op jit(solution)/shard_map/ppermute | solution.py:209
  4.2 8.6 %collective-permute-start.1 = (f32[2,8,4]{2,1,0:T(8,128)S(1)}, f32[2,8,4]{2,1,0:T(8,128)S(1)}, u32[]{:S(2)}, u32[]{:S(2)}) collective-permute-start(f32[2,8,4]{2,1,0:T(8,128)S(1)} %get-tuple-element.52), channel_id=1, source_target_pairs={{1,0},{2,1},{3,2},{4,3},{5,4},{6,5},{7,6},{8,7},{9,8},{10,9},{11,1... | collective-permute-start | bytes 776 | tf_op jit(solution)/shard_map/ppermute | solution.py:210
  52.1 10.9 %all-to-all-start.1 = ((f32[4,2,16,8,128]{4,3,2,1,0:T(8,128)}), f32[4,2,16,8,128]{4,3,2,1,0:T(8,128)S(1)}, u32[]{:S(2)}, u32[]{:S(2)}) async-start(f32[4,2,16,8,128]{4,3,2,1,0:T(8,128)} %broadcast_in_dim.28), calls=%async_computation.1 | async-start | bytes 1048576 | tf_op jit(solution)/shard_map/all_to_all | solution.py:231
  63.0 1.3 copy-start.1
  64.3 3.8 %copy-start.13 = (f32[128,128]{1,0:T(8,128)S(1)}, f32[128,128]{1,0:T(8,128)}, u32[]{:S(2)}) copy-start(f32[128,128]{1,0:T(8,128)} %param.9) | copy-start | bytes 196612
  64.3 21.8 %all-to-all-start.2 = ((f32[4,2,4,11,8,128]{5,4,3,2,1,0:T(8,128)}), f32[4,2,4,11,8,128]{5,4,3,2,1,0:T(8,128)S(1)}, u32[]{:S(2)}, u32[]{:S(2)}) async-start(f32[4,2,4,11,8,128]{5,4,3,2,1,0:T(8,128)} %broadcast_in_dim.29), calls=%async_computation.2 | async-start | bytes 2883584 | tf_op jit(solution)/shard_map/all_to_all | solution.py:234
  71.5 11.2 %collective-permute-start.2 = (f32[4,64,128]{2,1,0:T(8,128)}, f32[4,64,128]{2,1,0:T(8,128)S(1)}, u32[]{:S(2)}, u32[]{:S(2)}) collective-permute-start(f32[4,64,128]{2,1,0:T(8,128)} %get-tuple-element.25), channel_id=1, source_target_pairs={{15,0},{0,128},{128,256},{256,384},{384,512},{512,640},{640,64},{6... | collective-permute-start | bytes 393224 | tf_op jit(solution)/shard_map/ppermute | solution.py:255
  79.3 6.8 %collective-permute-start.3 = (f32[4,64,128]{2,1,0:T(8,128)}, f32[4,64,128]{2,1,0:T(8,128)S(1)}, u32[]{:S(2)}, u32[]{:S(2)}) collective-permute-start(f32[4,64,128]{2,1,0:T(8,128)} %get-tuple-element.26), channel_id=1, source_target_pairs={{0,15},{128,0},{256,128},{384,256},{512,384},{640,512},{64,640},{1... | collective-permute-start | bytes 393224 | tf_op jit(solution)/shard_map/ppermute | solution.py:256
  82.7 3.4 %copy-start.3 = (f32[4,64,128]{2,1,0:T(8,128)}, f32[4,64,128]{2,1,0:T(8,128)S(1)}, u32[]{:S(2)}) copy-start(f32[4,64,128]{2,1,0:T(8,128)S(1)} %collective-permute-done.2.low_ref) | copy-start | bytes 393220
  86.1 0.7 copy-start.4
  86.1 1.2 copy-start
  91.3 11.9 %collective-permute-start.4 = (f32[4,64,128]{2,1,0:T(8,128)}, f32[4,64,128]{2,1,0:T(8,128)S(1)}, u32[]{:S(2)}, u32[]{:S(2)}) collective-permute-start(f32[4,64,128]{2,1,0:T(8,128)} %get-tuple-element.30), channel_id=1, source_target_pairs={{15,0},{0,128},{128,256},{256,384},{384,512},{512,640},{640,64},{6... | collective-permute-start | bytes 393224 | tf_op jit(solution)/shard_map/ppermute | solution.py:255
  100.4 6.5 %collective-permute-start.5 = (f32[4,64,128]{2,1,0:T(8,128)}, f32[4,64,128]{2,1,0:T(8,128)S(1)}, u32[]{:S(2)}, u32[]{:S(2)}) collective-permute-start(f32[4,64,128]{2,1,0:T(8,128)} %get-tuple-element.31), channel_id=1, source_target_pairs={{0,15},{128,0},{256,128},{384,256},{512,384},{640,512},{64,640},{1... | collective-permute-start | bytes 393224 | tf_op jit(solution)/shard_map/ppermute | solution.py:256
  103.2 3.7 %copy-start.5 = (f32[4,64,128]{2,1,0:T(8,128)}, f32[4,64,128]{2,1,0:T(8,128)S(1)}, u32[]{:S(2)}) copy-start(f32[4,64,128]{2,1,0:T(8,128)S(1)} %collective-permute-done.4.low_ref) | copy-start | bytes 393220
  106.9 0.7 copy-start.9
  111.6 6.4 %collective-permute-start.6 = (f32[4,64,128]{2,1,0:T(8,128)}, f32[4,64,128]{2,1,0:T(8,128)S(1)}, u32[]{:S(2)}, u32[]{:S(2)}) collective-permute-start(f32[4,64,128]{2,1,0:T(8,128)} %get-tuple-element.34), channel_id=1, source_target_pairs={{15,0},{0,128},{128,256},{256,384},{384,512},{512,640},{640,64},{6... | collective-permute-start | bytes 393224 | tf_op jit(solution)/shard_map/ppermute | solution.py:255
  115.1 6.5 %collective-permute-start.7 = (f32[4,64,128]{2,1,0:T(8,128)}, f32[4,64,128]{2,1,0:T(8,128)S(1)}, u32[]{:S(2)}, u32[]{:S(2)}) collective-permute-start(f32[4,64,128]{2,1,0:T(8,128)} %get-tuple-element.35), channel_id=1, source_target_pairs={{0,15},{128,0},{256,128},{384,256},{512,384},{640,512},{64,640},{1... | collective-permute-start | bytes 393224 | tf_op jit(solution)/shard_map/ppermute | solution.py:256
  117.9 3.7 %copy-start.6 = (f32[4,64,128]{2,1,0:T(8,128)}, f32[4,64,128]{2,1,0:T(8,128)S(1)}, u32[]{:S(2)}) copy-start(f32[4,64,128]{2,1,0:T(8,128)S(1)} %collective-permute-done.6.low_ref) | copy-start | bytes 393220
  121.6 0.7 copy-start.10
  126.3 6.2 %collective-permute-start.8 = (f32[4,64,128]{2,1,0:T(8,128)}, f32[4,64,128]{2,1,0:T(8,128)S(1)}, u32[]{:S(2)}, u32[]{:S(2)}) collective-permute-start(f32[4,64,128]{2,1,0:T(8,128)} %get-tuple-element.38), channel_id=1, source_target_pairs={{15,0},{0,128},{128,256},{256,384},{384,512},{512,640},{640,64},{6... | collective-permute-start | bytes 393224 | tf_op jit(solution)/shard_map/ppermute | solution.py:255
  128.8 6.5 %collective-permute-start.9 = (f32[4,64,128]{2,1,0:T(8,128)}, f32[4,64,128]{2,1,0:T(8,128)S(1)}, u32[]{:S(2)}, u32[]{:S(2)}) collective-permute-start(f32[4,64,128]{2,1,0:T(8,128)} %get-tuple-element.39), channel_id=1, source_target_pairs={{0,15},{128,0},{256,128},{384,256},{512,384},{640,512},{64,640},{1... | collective-permute-start | bytes 393224 | tf_op jit(solution)/shard_map/ppermute | solution.py:256
  132.5 2.8 %copy-start.7 = (f32[4,64,128]{2,1,0:T(8,128)}, f32[4,64,128]{2,1,0:T(8,128)S(1)}, u32[]{:S(2)}) copy-start(f32[4,64,128]{2,1,0:T(8,128)S(1)} %collective-permute-done.8.low_ref) | copy-start | bytes 393220
  135.3 0.7 copy-start.11
  140.0 6.2 %collective-permute-start.10 = (f32[4,64,128]{2,1,0:T(8,128)}, f32[4,64,128]{2,1,0:T(8,128)S(1)}, u32[]{:S(2)}, u32[]{:S(2)}) collective-permute-start(f32[4,64,128]{2,1,0:T(8,128)} %get-tuple-element.42), channel_id=1, source_target_pairs={{15,0},{0,128},{128,256},{256,384},{384,512},{512,640},{640,64},{6... | collective-permute-start | bytes 393224 | tf_op jit(solution)/shard_map/ppermute | solution.py:255
  142.7 7.0 %collective-permute-start.11 = (f32[4,64,128]{2,1,0:T(8,128)}, f32[4,64,128]{2,1,0:T(8,128)S(1)}, u32[]{:S(2)}, u32[]{:S(2)}) collective-permute-start(f32[4,64,128]{2,1,0:T(8,128)} %get-tuple-element.43), channel_id=1, source_target_pairs={{0,15},{128,0},{256,128},{384,256},{512,384},{640,512},{64,640},{1... | collective-permute-start | bytes 393224 | tf_op jit(solution)/shard_map/ppermute | solution.py:256
  146.2 3.5 %copy-start.8 = (f32[4,64,128]{2,1,0:T(8,128)}, f32[4,64,128]{2,1,0:T(8,128)S(1)}, u32[]{:S(2)}) copy-start(f32[4,64,128]{2,1,0:T(8,128)S(1)} %collective-permute-done.10.low_ref) | copy-start | bytes 393220
  149.6 0.7 copy-start.12
  154.1 5.4 %copy-start.14 = (s32[4,1,2048]{2,1,0:T(1,128)S(1)}, s32[4,1,2048]{2,1,0:T(1,128)}, u32[]{:S(2)}) copy-start(s32[4,1,2048]{2,1,0:T(1,128)} %param.10) | copy-start | bytes 98308
  154.1 6.0 %copy-start.16 = (s32[1,1,16]{2,1,0:T(1,128)S(1)}, s32[1,1,16]{2,1,0:T(1,128)}, u32[]{:S(2)}) copy-start(s32[1,1,16]{2,1,0:T(1,128)} %param.12) | copy-start | bytes 196
  154.1 6.1 %copy-start.15 = (f32[4,1,2048]{2,1,0:T(1,128)S(1)}, f32[4,1,2048]{2,1,0:T(1,128)}, u32[]{:S(2)}) copy-start(f32[4,1,2048]{2,1,0:T(1,128)} %param.11) | copy-start | bytes 98308
  155.9 25.3 %all-to-all-start.3 = ((f32[12,11,8,128]{3,2,1,0:T(8,128)}), f32[12,11,8,128]{3,2,1,0:T(8,128)S(1)}, u32[]{:S(2)}, u32[]{:S(2)}) async-start(f32[12,11,8,128]{3,2,1,0:T(8,128)} %bitcast.19), calls=%async_computation.3 | async-start | bytes 1081344 | tf_op jit(solution)/shard_map/all_to_all | solution.py:275
  181.2 0.8 copy-start.2

commit v2 on v1

v2 whole, which is shorter than its diff:
```python
import functools

import jax
import jax.numpy as jnp
from jax import lax
from jax.experimental import pallas as pl
from jax.experimental.pallas import tpu as pltpu
from jax.sharding import Mesh
from jax.sharding import PartitionSpec as P

STEPS = 4
REACH = 2 * STEPS
WIDE = 11
LANE_B = 32

mixing_rate = 0.15

SMEM = functools.partial(pl.BlockSpec, memory_space=pltpu.SMEM)
VMEM = functools.partial(pl.BlockSpec, memory_space=pltpu.VMEM)


def params(mebibytes):
    return pltpu.CompilerParams(vmem_limit_bytes=mebibytes << 20)


def cost(flops, moved):
    return pl.CostEstimate(flops=flops, bytes_accessed=moved, transcendentals=0)


def starts_of(width, planes):
    return [width * j // planes for j in range(planes + 1)]


def halves(x):
    high = x.astype(jnp.bfloat16)
    low = (x - high.astype(jnp.float32)).astype(jnp.bfloat16)
    return high, low


def cut_kernel(planes, odd_ref, forcing_ref, rates_ref, around_ref, out_ref, turned):
    levels, width_x, width_y = forcing_ref.shape
    odd = odd_ref[0]
    for x in range(width_x):
        turned[:, x, :] = forcing_ref[:, x, :].T
    whole = 2 * width_y
    lane = lax.broadcasted_iota(jnp.int32, (width_x, whole), 1)
    east_all = jnp.concatenate([rates_ref[0], around_ref[0]], axis=1)
    north_all = jnp.concatenate([rates_ref[1], around_ref[1]], axis=1)
    for j, start in enumerate(starts_of(width_y, planes)[:-1]):
        place = jnp.where(odd == 1, planes - 1 - j, j)
        out_ref[place, 0:WIDE] = turned[start : start + WIDE]
        offset = REACH - start
        east = pltpu.roll(east_all, (whole + offset) % whole, 1)
        north = pltpu.roll(north_all, (whole + LANE_B + offset) % whole, 1)
        both = jnp.where(lane < LANE_B, east, north)
        out_ref[place, WIDE] = both[:, :levels]


def edges(size, up_ref, down_ref, state_ref, forcing_ref=None):
    depth = REACH if forcing_ref is not None else STEPS
    down_ref[0:depth] = state_ref[0:depth]
    up_ref[0:depth] = state_ref[pl.ds(size - depth, depth)]
    if forcing_ref is not None:
        down_ref[depth:] = forcing_ref[0:STEPS]
        up_ref[depth:] = forcing_ref[pl.ds(size - STEPS, STEPS)]


def spread_kernel(size_ref, first_ref, own_ref, next_ref, up_ref, down_ref, rates_ref):
    nx, nz, rows, part, _ = first_ref.shape
    for z in range(nz):
        for x in range(nx):
            at = (z * nx + x) * part
            own_ref[:, at : at + part, :] = first_ref[x, z, 0:WIDE]
            next_ref[:, at : at + part, :] = first_ref[x, z, WIDE : 2 * WIDE]
            for s in range(rows - 2 * WIDE):
                rates_ref[s, at : at + part, :] = first_ref[x, z, 2 * WIDE + s]
    edges(size_ref[0], up_ref, down_ref, own_ref, next_ref)


def fill_window(window, reach, size, own, low, high):
    window[0:reach] = low
    window[reach : reach + WIDE] = own
    window[reach + WIDE + reach - 1] = jnp.zeros(window.shape[1:], jnp.float32)
    window[pl.ds(reach + size, reach)] = high


def fill_table(table, mix_ref):
    levels = mix_ref.shape[0]
    mix_high, mix_low = halves(mix_ref[...])
    table[0:levels] = mix_high
    table[levels : 2 * levels] = mix_high
    table[2 * levels :] = mix_low


def advance(bufs, first, end, lane, rate, rate_refs, table):
    _, whole_x, levels = bufs[0].shape
    to_east, to_west, to_north, to_south = rate_refs
    shape = (whole_x, levels)
    for y in range(first + 1, end - 1):
        east = jnp.broadcast_to(rate[:, lane + y : lane + y + 1], shape)
        north = jnp.broadcast_to(rate[:, LANE_B + lane + y : LANE_B + lane + y + 1], shape)
        to_east[y] = mixing_rate + east
        to_west[y] = mixing_rate - east
        to_north[y] = mixing_rate + north
        to_south[y] = mixing_rate - north
    for step in range(STEPS):
        source, target = bufs[step % 2], bufs[(step + 1) % 2]
        low, high = first + step + 1, end - step - 1
        for y in range(low, high):
            centre = source[y]
            eastern = pltpu.roll(centre, whole_x - 1, 0)
            western = pltpu.roll(centre, 1, 0)
            across = to_east[y] * eastern + to_west[y] * western
            along = to_north[y] * source[y + 1] + to_south[y] * source[y - 1]
            target[y] = (1.0 - 4.0 * mixing_rate) * centre + (across + along)
        count = high - low
        z = target[low:high].reshape(count * whole_x, levels)
        z_high, z_low = halves(z)
        z = z + jnp.dot(
            jnp.concatenate([z_high, z_low, z_high], axis=1),
            table[...],
            preferred_element_type=jnp.float32,
        )
        target[low:high] = z.reshape(count, whole_x, levels)


def take_part(part_ref, window, reach, x_place):
    nz, _, part, _ = part_ref.shape
    whole_x = window.shape[1]
    for z in range(nz):
        at = pl.multiple_of(z * (whole_x // nz) + x_place * part, part)
        part_ref[z] = window[reach : reach + WIDE, pl.ds(at, part), :]


def gather_x(out_ref, later_ref, index):
    nx, nz, _, _, part, _ = later_ref.shape
    for z in range(nz):
        for x in range(nx):
            at = (z * nx + x) * part
            out_ref[:, at : at + part, :] = later_ref[x, z, index]


def two_slots(size_ref, own_ref, mid_ref, low_ref, high_ref, rates, mix_ref, parts, scratch):
    ping, pong, force, table = scratch[:4]
    coefficients = scratch[4:]
    size, x_place = size_ref[0], size_ref[1]
    fill_window(ping, REACH, size, own_ref[...], low_ref[0:REACH], high_ref[0:REACH])
    fill_window(force, STEPS, size, mid_ref[...], low_ref[REACH:], high_ref[REACH:])
    fill_table(table, mix_ref)
    rows = WIDE + 2 * REACH
    advance((ping, pong), 0, rows, 0, rates[0], coefficients, table)
    take_part(parts[0], ping, REACH, x_place)
    ping[STEPS : rows - STEPS] = ping[STEPS : rows - STEPS] + force[...]
    advance((ping, pong), STEPS, rows - STEPS, 0, rates[1], coefficients, table)
    take_part(parts[1], ping, REACH, x_place)
    return ping[REACH : REACH + WIDE]


def early_kernel(
    size_ref, own_ref, mid_ref, low_ref, high_ref, rates_ref, mix_ref, later_ref,
    next_ref, mid_next_ref, end_next_ref, up_ref, down_ref, part_a, part_b, *scratch,
):
    gather_x(next_ref, later_ref, 0)
    gather_x(mid_next_ref, later_ref, 1)
    gather_x(end_next_ref, later_ref, 2)
    moved = two_slots(
        size_ref, own_ref, mid_ref, low_ref, high_ref, (rates_ref.at[0], rates_ref.at[1]),
        mix_ref, (part_a, part_b), scratch,
    )
    next_ref[...] = next_ref[...] + moved
    edges(size_ref[0], up_ref, down_ref, next_ref, mid_next_ref)


def middle_kernel(
    size_ref, own_ref, mid_ref, low_ref, high_ref, rates_ref, mix_ref, end_ref,
    next_ref, up_ref, down_ref, part_a, part_b, *scratch,
):
    moved = two_slots(
        size_ref, own_ref, mid_ref, low_ref, high_ref, (rates_ref.at[2], rates_ref.at[3]),
        mix_ref, (part_a, part_b), scratch,
    )
    next_ref[...] = end_ref[...] + moved
    edges(size_ref[0], up_ref, down_ref, next_ref)


def late_kernel(
    size_ref, own_ref, low_ref, high_ref, rates_ref, mix_ref, *rest
):
    kept, home_ref, (ping, pong, table) = rest[:4], rest[4], rest[5:8]
    coefficients = rest[8:]
    fill_window(ping, STEPS, size_ref[0], own_ref[...], low_ref[...], high_ref[...])
    fill_table(table, mix_ref)
    nz = home_ref.shape[0]
    home_ref[:, 0] = jnp.zeros_like(kept[0])
    for index, part in enumerate(kept):
        home_ref[:, index + 1] = part[...]
    advance(
        (ping, pong), 0, WIDE + 2 * STEPS, STEPS, rates_ref.at[4], coefficients, table
    )
    take_part(home_ref.at[:, 5], ping, STEPS, size_ref[1])


def table_kernel(cells_ref, weights_ref, out_ref):
    _, columns, wide = out_ref.shape
    capacity = wide // 2
    column = lax.broadcasted_iota(jnp.int32, (columns, capacity), 0)
    for owner in range(out_ref.shape[0]):
        at = slice(owner * capacity, (owner + 1) * capacity)
        table = None
        for corner in range(cells_ref.shape[0]):
            cell = cells_ref[corner : corner + 1, at]
            weight = weights_ref[corner : corner + 1, at]
            term = jnp.where(column == cell, weight, 0.0)
            table = term if table is None else table + term
        high, low = halves(table)
        out_ref[owner, :, :capacity] = high
        out_ref[owner, :, capacity:] = low


def observe_kernel(
    planes, odd_ref, strips_ref, forcing_ref, table_ref, state_ref, out_ref, turned, split
):
    levels, width_x, width_y = forcing_ref.shape

    @pl.when(pl.program_id(0) == 0)
    def _():
        odd = odd_ref[0]
        starts = starts_of(width_y, planes)
        for j in range(planes):
            place = jnp.where(odd == 1, planes - 1 - j, j)
            turned[starts[j] : starts[j] + WIDE] = strips_ref[place]
        for x in range(width_x):
            value = turned[:, x, :].T + forcing_ref[:, x, :]
            state_ref[:, x, :] = value
            high, low = halves(value)
            split[0:levels, x * width_y : (x + 1) * width_y] = high
            split[levels:, x * width_y : (x + 1) * width_y] = low

    capacity = out_ref.shape[2]
    for owner in range(out_ref.shape[0]):
        both = jnp.dot(split[...], table_ref[owner], preferred_element_type=jnp.float32)
        out_ref[owner] = both[:levels, :capacity] + (
            both[:levels, capacity:] + both[levels:, :capacity]
        )


def channel_kernel(table_ref, profile_ref, out_ref):
    table_high, table_low = halves(table_ref[...])
    left = jnp.concatenate([table_high, table_low, table_high], axis=1)
    blocks, _, capacity = profile_ref.shape
    group = 4
    for block in range(0, blocks, group):
        value = jnp.concatenate([profile_ref[block + i] for i in range(group)], axis=1)
        high, low = halves(value)
        right = jnp.concatenate([high, high, low], axis=0)
        out_ref[:, block * capacity : (block + group) * capacity] = jnp.dot(
            left, right, preferred_element_type=jnp.float32
        )


def f32(*shape):
    return jax.ShapeDtypeStruct(shape, jnp.float32)


def local(forcing, winds, mixing, observation_columns, obs_weights, obs_counts, jacobian):
    slots = lax.axis_size("slot")
    halves_z = lax.axis_size("zhi")
    parts_x = lax.axis_size("x")
    owners = lax.axis_size("obs")
    planes = slots * halves_z
    rounds = slots - 1
    block = forcing[0]
    levels, width_x, width_y = block.shape
    whole_x = width_x * parts_x * halves_z
    starts = starts_of(width_y, planes)

    place_o = lax.axis_index("obs")
    place_z = lax.axis_index("zhi") * slots + lax.axis_index("slot")
    odd = (place_o % 2).astype(jnp.int32)
    strip = jnp.where(odd == 1, planes - 1 - place_z, place_z)
    size = (width_y * (strip + 1)) // planes - (width_y * strip) // planes
    odd = odd.reshape(1)
    sizes = jnp.stack([size.astype(jnp.int32), lax.axis_index("x").astype(jnp.int32)])

    order = []
    for o in range(owners):
        along = range(planes) if o % 2 == 0 else range(planes - 1, -1, -1)
        order += [((z % slots) * halves_z + z // slots) * owners + o for z in along]
    upward = [(order[i - 1], order[i]) for i in range(len(order))]
    downward = [(target, source) for source, target in upward]
    chain = ("slot", "zhi", "obs")

    rates = winds[:, 0]
    ring = [(i, (i + 1) % owners) for i in range(owners)]
    back = [(target, source) for source, target in ring]
    rates_low = lax.ppermute(rates[:, :, width_y - REACH :], "obs", ring)
    rates_high = lax.ppermute(rates[:, :, :REACH], "obs", back)
    around = jnp.concatenate(
        [rates_high, jnp.zeros((2, width_x, width_y - 2 * REACH), jnp.float32), rates_low], axis=2
    )

    cut = pl.pallas_call(
        functools.partial(cut_kernel, planes),
        out_shape=f32(planes, WIDE + 1, width_x, levels),
        in_specs=[SMEM()] + [VMEM()] * 3,
        out_specs=VMEM(),
        scratch_shapes=[pltpu.VMEM((width_y, width_x, levels), jnp.float32)],
        compiler_params=params(8),
        cost_estimate=cost(4000000, 1100000),
        name="cut",
    )(odd, block, rates, around)
    strips = lax.all_to_all(cut, ("zhi", "slot"), 0, 0, tiled=True)
    strips = strips.reshape(halves_z, slots, WIDE + 1, width_x, levels)
    first = jnp.concatenate(
        [strips[:, 0, :WIDE], strips[:, 1, :WIDE], strips[:, :rounds, WIDE]], axis=1
    )
    later = strips[:, 2:rounds, :WIDE]
    first = lax.all_to_all(
        jnp.broadcast_to(first, (parts_x,) + first.shape), "x", 0, 0, tiled=True
    ).reshape((parts_x,) + first.shape)
    later = lax.all_to_all(
        jnp.broadcast_to(later, (parts_x,) + later.shape), "x", 0, 0, tiled=True
    ).reshape((parts_x,) + later.shape)

    strip = f32(WIDE, whole_x, levels)
    far = pltpu.HBM((WIDE, whole_x, levels), jnp.float32)
    edge = f32(REACH + STEPS, whole_x, levels)
    last_edge = f32(STEPS, whole_x, levels)
    part = f32(halves_z, WIDE, width_x, levels)
    own, mid, up, down, rates = pl.pallas_call(
        spread_kernel,
        out_shape=(far, far, edge, edge, f32(rounds, whole_x, levels)),
        in_specs=[SMEM(), VMEM()],
        out_specs=(VMEM(),) * 5,
        compiler_params=params(8),
        cost_estimate=cost(1000000, 2500000),
        name="spread",
    )(sizes, first)

    turned_mixing = mixing.T
    table = pltpu.VMEM((3 * levels, levels), jnp.bfloat16)

    def window(rows):
        return pltpu.VMEM((rows, whole_x, levels), jnp.float32)

    long = WIDE + 2 * REACH
    short = WIDE + 2 * STEPS
    long_scratch = [window(long)] * 2 + [window(short), table] + [window(long)] * 4
    short_scratch = [window(short)] * 2 + [table] + [window(short)] * 4

    low = lax.ppermute(up, chain, upward)
    high = lax.ppermute(down, chain, downward)
    own, mid = (pltpu.with_memory_space_constraint(x, pltpu.HBM) for x in (own, mid))
    own, mid, end, up, down, *kept = pl.pallas_call(
        early_kernel,
        out_shape=(strip, strip, strip, edge, edge, part, part),
        in_specs=[SMEM()] + [VMEM()] * 7,
        out_specs=(VMEM(),) * 7,
        scratch_shapes=long_scratch,
        compiler_params=params(24),
        cost_estimate=cost(900000000, 4000000),
        name="early",
    )(sizes, own, mid, low, high, rates, turned_mixing, later)
    low = lax.ppermute(up, chain, upward)
    high = lax.ppermute(down, chain, downward)
    own, up, down, *kept[2:] = pl.pallas_call(
        middle_kernel,
        out_shape=(strip, last_edge, last_edge, part, part),
        in_specs=[SMEM()] + [VMEM()] * 7,
        out_specs=(VMEM(),) * 5,
        scratch_shapes=long_scratch,
        compiler_params=params(24),
        cost_estimate=cost(900000000, 4000000),
        name="middle",
    )(sizes, own, mid, low, high, rates, turned_mixing, end)
    low = lax.ppermute(up, chain, upward)
    high = lax.ppermute(down, chain, downward)
    home = pl.pallas_call(
        late_kernel,
        out_shape=f32(halves_z, slots, WIDE, width_x, levels),
        in_specs=[SMEM()] + [VMEM()] * 9,
        out_specs=VMEM(),
        scratch_shapes=short_scratch,
        compiler_params=params(24),
        cost_estimate=cost(400000000, 3000000),
        name="late",
    )(sizes, own, low, high, rates, turned_mixing, *kept)

    cells = observation_columns[:, 0]
    points, row_count = cells.shape
    capacity = row_count // owners
    live = lax.broadcasted_iota(jnp.int32, (owners, capacity), 1) < obs_counts[0, 0][:, None]
    weights = jnp.where(live.reshape(1, row_count), obs_weights[:, 0], 0.0)
    home, weights = lax.optimization_barrier((home, weights))
    home = home.reshape(planes, WIDE, width_x, levels)
    home = lax.all_to_all(home, ("zhi", "slot"), 0, 0, tiled=True)

    columns = width_x * width_y
    group = 2
    tables = pl.pallas_call(
        table_kernel,
        out_shape=pltpu.HBM((owners, columns, 2 * capacity), jnp.bfloat16),
        grid=(owners // group,),
        in_specs=[pl.BlockSpec((points, group * capacity), lambda q: (0, q))] * 2,
        out_specs=pl.BlockSpec((group, columns, 2 * capacity), lambda q: (q, 0, 0)),
        compiler_params=params(20),
        cost_estimate=cost(1000000000, 8500000),
        name="table",
    )(cells, weights)
    tables = pltpu.with_memory_space_constraint(tables, pltpu.HBM)
    state, profile = pl.pallas_call(
        functools.partial(observe_kernel, planes),
        out_shape=(f32(levels, width_x, width_y), f32(owners, levels, capacity)),
        grid=(owners // group,),
        in_specs=[
            SMEM(),
            pl.BlockSpec((planes, WIDE, width_x, levels), lambda q: (0, 0, 0, 0)),
            pl.BlockSpec((levels, width_x, width_y), lambda q: (0, 0, 0)),
            pl.BlockSpec((group, columns, 2 * capacity), lambda q: (q, 0, 0)),
        ],
        out_specs=(
            pl.BlockSpec((levels, width_x, width_y), lambda q: (0, 0, 0)),
            pl.BlockSpec((group, levels, capacity), lambda q: (q, 0, 0)),
        ),
        scratch_shapes=[
            pltpu.VMEM((width_y, width_x, levels), jnp.float32),
            pltpu.VMEM((2 * levels, columns), jnp.bfloat16),
        ],
        compiler_params=params(20),
        cost_estimate=cost(2000000000, 11000000),
        name="observe",
    )(odd, home, block, tables)

    profile = lax.all_to_all(profile, "obs", 0, 0, tiled=True)
    channels = jacobian.shape[2]
    radiance = pl.pallas_call(
        channel_kernel,
        out_shape=f32(channels, row_count),
        in_specs=[VMEM()] * 2,
        out_specs=VMEM(),
        compiler_params=params(12),
        cost_estimate=cost(200000000, 2200000),
        name="channel",
    )(jacobian[0, 0], profile)
    return (state[None], radiance[None])


def solution(mesh):
    slots, tiles, owners = (mesh.shape[name] for name in ("slot", "tile", "obs"))
    fine = Mesh(
        mesh.devices.reshape(slots, 2, tiles // 2, owners), ("slot", "zhi", "x", "obs")
    )
    tile = ("zhi", "x")
    return jax.shard_map(
        local,
        mesh=fine,
        in_specs=(
            P("slot", None, tile, "obs"),
            P(None, "slot", tile, "obs"),
            P(),
            P(None, "slot", tile + ("obs",)),
            P(None, "slot", tile + ("obs",)),
            P("slot", tile + ("obs",), None),
            P("slot", "obs", None, None),
        ),
        out_specs=(P("slot", None, tile, "obs"), P("slot", None, tile + ("obs",))),
        check_vma=False,
    )
```

time: 241 us -> 201 us (0.83)
  local copies, waits for them, and re-layouts: 15.9 us -> 4.88 us
  starting transfers between devices: 58.5 us -> 48.3 us
  Pallas kernels: 40.4 us -> 32 us
  blocking collectives: 75.8 us -> 69.3 us
  other arithmetic: 2.73 us -> 0.26 us
    unnamed x41 -> x18, local copies, waits for them, and re-layouts: 9.56 us -> 1.87 us
    all_to_all x1, waiting for transfers between devices: 20.4 us -> 14.5 us  [local(): home = lax.all_to_all(home, ('zhi', 'slot'), 0, 0, tiled=True)]
    all_to_all x1, blocking collectives: 34.5 us -> 28.8 us  [local(): strips = lax.all_to_all(cut, ('zhi', 'slot'), 0, 0, tiled=True)]
    ppermute x5 -> x3, waiting for transfers between devices: 0.03 us -> 5.7 us  [local(): low = lax.ppermute(up, chain, upward)]
    ppermute x5 -> x3, starting transfers between devices: 11.1 us -> 5.94 us  [local(): high = lax.ppermute(down, chain, downward)]
    ppermute x5 -> x3, starting transfers between devices: 25.6 us -> 20.7 us  [local(): low = lax.ppermute(up, chain, upward)]
    pallas_call x7 -> x6, Pallas kernels: 25.8 us -> 22.5 us  [the longest x1 7.32 us: local(): pl.pallas_call(table_kernel, out_shape=pltpu.HBM((owners, columns, 2 * ca...]
    pallas_call x1, Pallas kernels: 12.1 us -> 8.84 us  [local(): pl.pallas_call(functools.partial(observe_kernel, planes), out_shape=(f32(...]
  transfers between devices with their start and end apart: 15 -> 11, of which waited for: 9 -> 9; matrix products, arithmetic and copies ran while one was open for 3% -> 0% of each run, Pallas kernels for 1% -> 4%
where the time goes in v2:
time: 201 us; the launch traced here: 200 us
  blocking collectives  69.3 us (34%)
  starting transfers between devices  48.3 us (24%)
  waiting for transfers between devices  44.4 us (22%)
  Pallas kernels  32 us (16%)
  local copies, waits for them, and re-layouts  4.88 us (2%)
    all_to_all x1, blocking collectives, local(): profile = lax.all_to_all(profile, 'obs', 0, 0, tiled=True)  40.6 us
    all_to_all x1, blocking collectives, local(): strips = lax.all_to_all(cut, ('zhi', 'slot'), 0, 0, tiled=True)  28.8 us
    ppermute x3, starting transfers between devices, local(): low = lax.ppermute(up, chain, upward)  20.7 us
    all_to_all x1, waiting for transfers between devices, local(): home = lax.all_to_all(home, ('zhi', 'slot'), 0, 0, tiled=True)  14.5 us
    ppermute x3, waiting for transfers between devices, local(): high = lax.ppermute(down, chain, downward)  14.2 us
    ppermute x1, starting transfers between devices, local(): rates_high = lax.ppermute(rates[:, :, :REACH], 'obs', back)  10.5 us
    all_to_all x1, waiting for transfers between devices, local(): lax.all_to_all(jnp.broadcast_to(first, (parts_x,) + first.shape), 'x', 0,...  8.84 us
    pallas_call x1, Pallas kernels, local(): pl.pallas_call(functools.partial(observe_kernel, planes), out_shape=(f32(...  8.84 us
  transfers between devices with their start and end apart: 11, of which 9 were waited for; matrix products, arithmetic and copies ran while one was open for 0% of the time, Pallas kernels for 4%

profile of v2, /device:TPU:1, one launch (start us, length us, event | category | flops | bytes accessed | tf_op | source)
XLA Modules:
  0.0 200.1 jit_solution(2928623618307457765)
XLA Ops:
  0.6 0.8 fusion.1
  1.5 10.5 %collective-permute-start = (f32[2,8,8]{2,1,0:T(8,128)S(1)}, f32[2,8,8]{2,1,0:T(8,128)S(1)}, u32[]{:S(2)}, u32[]{:S(2)}) collective-permute-start(f32[2,8,8]{2,1,0:T(8,128)S(1)} %get-tuple-element.46), channel_id=1, source_target_pairs={{1,0},{2,1},{3,2},{4,3},{5,4},{6,5},{7,6},{8,7},{9,8},{10,9},{11,1... | collective-permute-start | bytes 1544 | tf_op jit(solution)/shard_map/ppermute | solution.py:297
  12.0 0.7 collective-permute-done
  13.2 1.0 copy-done
  14.2 0.7 copy-done.2
  15.6 28.8 %all_to_all.25 = f32[12,12,8,128]{3,2,1,0:T(8,128)S(1)} all-to-all(f32[12,12,8,128]{3,2,1,0:T(8,128)S(1)} %cut.1), channel_id=1, replica_groups=mesh['slot'=6,'zhi'=2,'x'=4,'obs'=16] {'zhi','slot'}, dimensions={0} | all-to-all | bytes 1179648 | tf_op jit(solution)/shard_map/all_to_all | solution.py:312
  44.4 1.0 broadcast_in_dim.28
  45.4 4.0 %all-to-all-start.1 = ((f32[4,2,27,8,128]{4,3,2,1,0:T(8,128)}), f32[4,2,27,8,128]{4,3,2,1,0:T(8,128)S(1)}, u32[]{:S(2)}, u32[]{:S(2)}) async-start(f32[4,2,27,8,128]{4,3,2,1,0:T(8,128)} %broadcast_in_dim.28), calls=%async_computation.1 | async-start | bytes 1769472 | tf_op jit(solution)/shard_map/all_to_all | solution.py:318
  49.4 8.8 %all-to-all-done.1.first_ref = f32[4,2,27,8,128]{4,3,2,1,0:T(8,128)S(1)} async-done(((f32[4,2,27,8,128]{4,3,2,1,0:T(8,128)}), f32[4,2,27,8,128]{4,3,2,1,0:T(8,128)S(1)}, u32[]{:S(2)}, u32[]{:S(2)}) %all-to-all-start.1) | async-done | bytes 884768 | tf_op jit(solution)/shard_map/all_to_all | solution.py:318
  58.2 1.1 broadcast_in_dim.29
  59.3 3.6 %all-to-all-start.2 = ((f32[4,2,3,11,8,128]{5,4,3,2,1,0:T(8,128)}), f32[4,2,3,11,8,128]{5,4,3,2,1,0:T(8,128)S(1)}, u32[]{:S(2)}, u32[]{:S(2)}) async-start(f32[4,2,3,11,8,128]{5,4,3,2,1,0:T(8,128)} %broadcast_in_dim.29), calls=%async_computation.2 | async-start | bytes 2162688 | tf_op jit(solution)/shard_map/all_to_all | solution.py:321
  63.1 1.5 spread.1
  64.6 12.2 %collective-permute-start.2 = (f32[12,64,128]{2,1,0:T(8,128)S(1)}, f32[12,64,128]{2,1,0:T(8,128)S(1)}, u32[]{:S(2)}, u32[]{:S(2)}) collective-permute-start(f32[12,64,128]{2,1,0:T(8,128)S(1)} %get-tuple-element.25), channel_id=1, source_target_pairs={{15,0},{0,128},{128,256},{256,384},{384,512},{512,640},{640,64},{6... | collective-permute-start | bytes 1179656 | tf_op jit(solution)/shard_map/ppermute | solution.py:351
  76.9 1.9 collective-permute-start.3
  78.9 2.7 %collective-permute-done.2.low_ref = f32[12,64,128]{2,1,0:T(8,128)S(1)} collective-permute-done((f32[12,64,128]{2,1,0:T(8,128)S(1)}, f32[12,64,128]{2,1,0:T(8,128)S(1)}, u32[]{:S(2)}, u32[]{:S(2)}) %collective-permute-start.2) | collective-permute-done | bytes 393248 | tf_op jit(solution)/shard_map/ppermute | solution.py:351
  81.6 5.6 %collective-permute-done.3.high_ref = f32[12,64,128]{2,1,0:T(8,128)S(1)} collective-permute-done((f32[12,64,128]{2,1,0:T(8,128)S(1)}, f32[12,64,128]{2,1,0:T(8,128)S(1)}, u32[]{:S(2)}, u32[]{:S(2)}) %collective-permute-start.3) | collective-permute-done | bytes 393248 | tf_op jit(solution)/shard_map/ppermute | solution.py:352
  87.1 5.0 %early.1 = (f32[11,64,128]{2,1,0:T(8,128)S(1)}, f32[11,64,128]{2,1,0:T(8,128)S(1)}, f32[11,64,128]{2,1,0:T(8,128)S(1)}, f32[12,64,128]{2,1,0:T(8,128)S(1)}, f32[...) custom-call(s32[2]{0:T(128)S(1)} %pad_add_fusion.size_ref, ...), custom_call_target="tpu_custom_call" | custom-call | flops 900000000 | bytes 4000000 | tf_op jit(solution)/shard_map/early/pallas_call | solution.py:354
  92.1 4.2 %collective-permute-start.4 = (f32[12,64,128]{2,1,0:T(8,128)S(1)}, f32[12,64,128]{2,1,0:T(8,128)S(1)}, u32[]{:S(2)}, u32[]{:S(2)}) collective-permute-start(f32[12,64,128]{2,1,0:T(8,128)S(1)} %get-tuple-element.30), channel_id=1, source_target_pairs={{15,0},{0,128},{128,256},{256,384},{384,512},{512,640},{640,64},{6... | collective-permute-start | bytes 1179656 | tf_op jit(solution)/shard_map/ppermute | solution.py:364
  96.4 1.9 collective-permute-start.5
  98.4 3.0 %collective-permute-done.4.low_ref = f32[12,64,128]{2,1,0:T(8,128)S(1)} collective-permute-done((f32[12,64,128]{2,1,0:T(8,128)S(1)}, f32[12,64,128]{2,1,0:T(8,128)S(1)}, u32[]{:S(2)}, u32[]{:S(2)}) %collective-permute-start.4) | collective-permute-done | bytes 393248 | tf_op jit(solution)/shard_map/ppermute | solution.py:364
  101.4 4.6 %collective-permute-done.5.high_ref = f32[12,64,128]{2,1,0:T(8,128)S(1)} collective-permute-done((f32[12,64,128]{2,1,0:T(8,128)S(1)}, f32[12,64,128]{2,1,0:T(8,128)S(1)}, u32[]{:S(2)}, u32[]{:S(2)}) %collective-permute-start.5) | collective-permute-done | bytes 393248 | tf_op jit(solution)/shard_map/ppermute | solution.py:365
  106.0 4.4 %middle.1 = (f32[11,64,128]{2,1,0:T(8,128)S(1)}, f32[4,64,128]{2,1,0:T(8,128)S(1)}, f32[4,64,128]{2,1,0:T(8,128)S(1)}, f32[2,11,8,128]{3,2,1,0:T(8,128)S(1)}, f32[2,11,8,128]{3,2,1,0:T(8,128)S(1)}) custom-call(s32[2]{0:T(128)S(1)} %pad_add_fusion.size_ref, f32[11,64,128]{2,1,0:T(8,128)S(1)} %get-tuple-element.28.own_ref, ...), custom_call_target="tpu_custom_call" | custom-call | flops 900000000 | bytes 4000000 | tf_op jit(solution)/shard_map/middle/pallas_call | solution.py:366
  110.3 4.2 %collective-permute-start.6 = (f32[4,64,128]{2,1,0:T(8,128)S(1)}, f32[4,64,128]{2,1,0:T(8,128)S(1)}, u32[]{:S(2)}, u32[]{:S(2)}) collective-permute-start(f32[4,64,128]{2,1,0:T(8,128)S(1)} %get-tuple-element.34), channel_id=1, source_target_pairs={{15,0},{0,128},{128,256},{256,384},{384,512},{512,640},{640,64},{6... | collective-permute-start | bytes 393224 | tf_op jit(solution)/shard_map/ppermute | solution.py:376
  114.6 2.1 %collective-permute-start.7 = (f32[4,64,128]{2,1,0:T(8,128)S(1)}, f32[4,64,128]{2,1,0:T(8,128)S(1)}, u32[]{:S(2)}, u32[]{:S(2)}) collective-permute-start(f32[4,64,128]{2,1,0:T(8,128)S(1)} %get-tuple-element.35), channel_id=1, source_target_pairs={{0,15},{128,0},{256,128},{384,256},{512,384},{640,512},{64,640},{1... | collective-permute-start | bytes 393224 | tf_op jit(solution)/shard_map/ppermute | solution.py:377
  116.7 4.1 %collective-permute-done.7.high_ref = f32[4,64,128]{2,1,0:T(8,128)S(1)} collective-permute-done((f32[4,64,128]{2,1,0:T(8,128)S(1)}, f32[4,64,128]{2,1,0:T(8,128)S(1)}, u32[]{:S(2)}, u32[]{:S(2)}) %collective-permute-start.7) | collective-permute-done | bytes 131104 | tf_op jit(solution)/shard_map/ppermute | solution.py:377
  120.9 2.9 %late.1 = f32[2,6,11,8,128]{4,3,2,1,0:T(8,128)} custom-call(s32[2]{0:T(128)S(1)} %pad_add_fusion.size_ref, f32[11,64,128]{2,1,0:T(8,128)S(1)} %get-tuple-element.33.own_ref, f32[4,64,128]{2,1,0:T(8,128)S(1)} %collective-permute-done.6.low_ref, f32[4,64,128]{2,1,0:T(8,128)S(1)} %collective-permute-done.7.high_ref, ...), custom_call_target="tpu_custom_call" | custom-call | flops 400000000 | bytes 3000000 | tf_op jit(solution)/shard_map/late/pallas_call | solution.py:378
  123.7 3.6 %all-to-all-start.3 = ((f32[12,11,8,128]{3,2,1,0:T(8,128)}), f32[12,11,8,128]{3,2,1,0:T(8,128)S(1)}, u32[]{:S(2)}, u32[]{:S(2)}) async-start(f32[12,11,8,128]{3,2,1,0:T(8,128)} %bitcast.12), calls=%async_computation.3 | async-start | bytes 1081344 | tf_op jit(solution)/shard_map/all_to_all | solution.py:396
  127.4 7.3 %table.1.table_ref = bf16[16,1024,256]{2,1,0:T(8,128)(2,1)} custom-call(s32[4,2048]{1,0:T(4,128)S(1)} %bitcast.32, f32[4,2048]{1,0:T(4,128)S(1)} %bitcast_select_fusion.weights_ref), custom_call_target="tpu_custom_call" | custom-call | flops 1000000000 | bytes 8500000 | tf_op jit(solution)/shard_map/table/pallas_call | solution.py:400
  134.7 14.5 %all-to-all-done.3.strips_ref = f32[12,11,8,128]{3,2,1,0:T(8,128)S(1)} async-done(((f32[12,11,8,128]{3,2,1,0:T(8,128)}), f32[12,11,8,128]{3,2,1,0:T(8,128)S(1)}, u32[]{:S(2)}, u32[]{:S(2)}) %all-to-all-start.3) | async-done | bytes 540704 | tf_op jit(solution)/shard_map/all_to_all | solution.py:396
  149.3 8.8 %observe.1 = (f32[128,8,128]{2,1,0:T(8,128)}, f32[16,128,128]{2,1,0:T(8,128)S(1)}) custom-call(s32[1]{0:T(128)} %bitcast.odd_ref, f32[12,11,8,128]{3,2,1,0:T(8,128)S(1)} %all-to-all-done.3.strips_ref, f32[128,8,128]{2,1,0:T(8,128)S(1)} %bitcast.28, bf16[16,1024,256]{2,1,0:T(8,128)(2,1)} %table.1.table_ref), custom_call_target="tpu_custom_call" | custom-call | flops 2000000000 | bytes 11000000 | tf_op jit(solution)/shard_map/observe/pallas_call | solution.py:411
  158.1 40.6 %all_to_all.26.profile_ref = f32[16,128,128]{2,1,0:T(8,128)S(1)} all-to-all(f32[16,128,128]{2,1,0:T(8,128)S(1)} %get-tuple-element.43), channel_id=1, replica_groups=mesh['slot'=6,'zhi'=2,'x'=4,'obs'=16] {'obs'}, dimensions={0} | all-to-all | bytes 2097152 | tf_op jit(solution)/shard_map/all_to_all | solution.py:434
  198.7 1.4 channel.1
  (31 shorter events, 1.5 us)
Async XLA Ops:
  1.5 11.3 %collective-permute-start = (f32[2,8,8]{2,1,0:T(8,128)S(1)}, f32[2,8,8]{2,1,0:T(8,128)S(1)}, u32[]{:S(2)}, u32[]{:S(2)}) collective-permute-start(f32[2,8,8]{2,1,0:T(8,128)S(1)} %get-tuple-element.46), channel_id=1, source_target_pairs={{1,0},{2,1},{3,2},{4,3},{5,4},{6,5},{7,6},{8,7},{9,8},{10,9},{11,1... | collective-permute-start | bytes 1544 | tf_op jit(solution)/shard_map/ppermute | solution.py:297
  12.0 1.2 collective-permute-start.1
  13.2 1.0 copy-start
  14.2 0.7 copy-start.2
  45.4 12.9 %all-to-all-start.1 = ((f32[4,2,27,8,128]{4,3,2,1,0:T(8,128)}), f32[4,2,27,8,128]{4,3,2,1,0:T(8,128)S(1)}, u32[]{:S(2)}, u32[]{:S(2)}) async-start(f32[4,2,27,8,128]{4,3,2,1,0:T(8,128)} %broadcast_in_dim.28), calls=%async_computation.1 | async-start | bytes 1769472 | tf_op jit(solution)/shard_map/all_to_all | solution.py:318
  59.3 19.5 %copy-start.4 = (f32[128,128]{1,0:T(8,128)S(1)}, f32[128,128]{1,0:T(8,128)}, u32[]{:S(2)}) copy-start(f32[128,128]{1,0:T(8,128)} %param.9) | copy-start | bytes 196612
  59.3 19.6 %all-to-all-start.2 = ((f32[4,2,3,11,8,128]{5,4,3,2,1,0:T(8,128)}), f32[4,2,3,11,8,128]{5,4,3,2,1,0:T(8,128)S(1)}, u32[]{:S(2)}, u32[]{:S(2)}) async-start(f32[4,2,3,11,8,128]{5,4,3,2,1,0:T(8,128)} %broadcast_in_dim.29), calls=%async_computation.2 | async-start | bytes 2162688 | tf_op jit(solution)/shard_map/all_to_all | solution.py:321
  64.6 16.9 %collective-permute-start.2 = (f32[12,64,128]{2,1,0:T(8,128)S(1)}, f32[12,64,128]{2,1,0:T(8,128)S(1)}, u32[]{:S(2)}, u32[]{:S(2)}) collective-permute-start(f32[12,64,128]{2,1,0:T(8,128)S(1)} %get-tuple-element.25), channel_id=1, source_target_pairs={{15,0},{0,128},{128,256},{256,384},{384,512},{512,640},{640,64},{6... | collective-permute-start | bytes 1179656 | tf_op jit(solution)/shard_map/ppermute | solution.py:351
  76.9 10.3 %collective-permute-start.3 = (f32[12,64,128]{2,1,0:T(8,128)S(1)}, f32[12,64,128]{2,1,0:T(8,128)S(1)}, u32[]{:S(2)}, u32[]{:S(2)}) collective-permute-start(f32[12,64,128]{2,1,0:T(8,128)S(1)} %get-tuple-element.26), channel_id=1, source_target_pairs={{0,15},{128,0},{256,128},{384,256},{512,384},{640,512},{64,640},{1... | collective-permute-start | bytes 1179656 | tf_op jit(solution)/shard_map/ppermute | solution.py:352
  87.1 11.2 %copy-start.7 = (s32[1,1,16]{2,1,0:T(1,128)S(1)}, s32[1,1,16]{2,1,0:T(1,128)}, u32[]{:S(2)}) copy-start(s32[1,1,16]{2,1,0:T(1,128)} %param.12) | copy-start | bytes 196
  92.1 9.3 %collective-permute-start.4 = (f32[12,64,128]{2,1,0:T(8,128)S(1)}, f32[12,64,128]{2,1,0:T(8,128)S(1)}, u32[]{:S(2)}, u32[]{:S(2)}) collective-permute-start(f32[12,64,128]{2,1,0:T(8,128)S(1)} %get-tuple-element.30), channel_id=1, source_target_pairs={{15,0},{0,128},{128,256},{256,384},{384,512},{512,640},{640,64},{6... | collective-permute-start | bytes 1179656 | tf_op jit(solution)/shard_map/ppermute | solution.py:364
  96.4 9.6 %collective-permute-start.5 = (f32[12,64,128]{2,1,0:T(8,128)S(1)}, f32[12,64,128]{2,1,0:T(8,128)S(1)}, u32[]{:S(2)}, u32[]{:S(2)}) collective-permute-start(f32[12,64,128]{2,1,0:T(8,128)S(1)} %get-tuple-element.31), channel_id=1, source_target_pairs={{0,15},{128,0},{256,128},{384,256},{512,384},{640,512},{64,640},{1... | collective-permute-start | bytes 1179656 | tf_op jit(solution)/shard_map/ppermute | solution.py:365
  106.0 10.7 %copy-start.5 = (f32[4,1,2048]{2,1,0:T(1,128)S(1)}, f32[4,1,2048]{2,1,0:T(1,128)}, u32[]{:S(2)}) copy-start(f32[4,1,2048]{2,1,0:T(1,128)} %param.11) | copy-start | bytes 98308
  110.3 6.4 %collective-permute-start.6 = (f32[4,64,128]{2,1,0:T(8,128)S(1)}, f32[4,64,128]{2,1,0:T(8,128)S(1)}, u32[]{:S(2)}, u32[]{:S(2)}) collective-permute-start(f32[4,64,128]{2,1,0:T(8,128)S(1)} %get-tuple-element.34), channel_id=1, source_target_pairs={{15,0},{0,128},{128,256},{256,384},{384,512},{512,640},{640,64},{6... | collective-permute-start | bytes 393224 | tf_op jit(solution)/shard_map/ppermute | solution.py:376
  114.6 6.3 %collective-permute-start.7 = (f32[4,64,128]{2,1,0:T(8,128)S(1)}, f32[4,64,128]{2,1,0:T(8,128)S(1)}, u32[]{:S(2)}, u32[]{:S(2)}) collective-permute-start(f32[4,64,128]{2,1,0:T(8,128)S(1)} %get-tuple-element.35), channel_id=1, source_target_pairs={{0,15},{128,0},{256,128},{384,256},{512,384},{640,512},{64,640},{1... | collective-permute-start | bytes 393224 | tf_op jit(solution)/shard_map/ppermute | solution.py:377
  120.8 6.5 %copy-start.6 = (s32[4,1,2048]{2,1,0:T(1,128)S(1)}, s32[4,1,2048]{2,1,0:T(1,128)}, u32[]{:S(2)}) copy-start(s32[4,1,2048]{2,1,0:T(1,128)} %param.10) | copy-start | bytes 98308
  123.7 25.5 %all-to-all-start.3 = ((f32[12,11,8,128]{3,2,1,0:T(8,128)}), f32[12,11,8,128]{3,2,1,0:T(8,128)S(1)}, u32[]{:S(2)}, u32[]{:S(2)}) async-start(f32[12,11,8,128]{3,2,1,0:T(8,128)} %bitcast.12), calls=%async_computation.3 | async-start | bytes 1081344 | tf_op jit(solution)/shard_map/all_to_all | solution.py:396
  127.4 21.9 %copy-start.1 = (f32[1,128,8,128]{3,2,1,0:T(8,128)S(1)}, f32[1,128,8,128]{3,2,1,0:T(8,128)}, u32[]{:S(2)}) copy-start(f32[1,128,8,128]{3,2,1,0:T(8,128)} %param.7) | copy-start | bytes 1572868
  158.1 40.6 %copy-start.3 = (f32[1,1,128,128]{3,2,1,0:T(8,128)S(1)}, f32[1,1,128,128]{3,2,1,0:T(8,128)}, u32[]{:S(2)}) copy-start(f32[1,1,128,128]{3,2,1,0:T(8,128)} %param.13) | copy-start | bytes 196612

commit v3 on v2

--- a/solution.py
+++ b/solution.py
@@ -37,23 +37,19 @@
     return high, low
 
 
-def cut_kernel(planes, odd_ref, forcing_ref, rates_ref, around_ref, out_ref, turned):
+def cut_kernel(planes, odd_ref, forcing_ref, rates_ref, out_ref, turned):
     levels, width_x, width_y = forcing_ref.shape
     odd = odd_ref[0]
     for x in range(width_x):
         turned[:, x, :] = forcing_ref[:, x, :].T
-    whole = 2 * width_y
-    lane = lax.broadcasted_iota(jnp.int32, (width_x, whole), 1)
-    east_all = jnp.concatenate([rates_ref[0], around_ref[0]], axis=1)
-    north_all = jnp.concatenate([rates_ref[1], around_ref[1]], axis=1)
+    lane = lax.broadcasted_iota(jnp.int32, (width_x, width_y), 1)
     for j, start in enumerate(starts_of(width_y, planes)[:-1]):
         place = jnp.where(odd == 1, planes - 1 - j, j)
         out_ref[place, 0:WIDE] = turned[start : start + WIDE]
-        offset = REACH - start
-        east = pltpu.roll(east_all, (whole + offset) % whole, 1)
-        north = pltpu.roll(north_all, (whole + LANE_B + offset) % whole, 1)
-        both = jnp.where(lane < LANE_B, east, north)
-        out_ref[place, WIDE] = both[:, :levels]
+        east = pltpu.roll(rates_ref[0], (width_y - start) % width_y, 1)
+        north = pltpu.roll(rates_ref[1], (width_y + WIDE - start) % width_y, 1)
+        both = jnp.where(lane < WIDE, east, north)
+        out_ref[place, WIDE] = jnp.where(lane < 2 * WIDE, both, 0.0)
 
 
 def edges(size, up_ref, down_ref, state_ref, forcing_ref=None):
@@ -61,8 +57,8 @@
     down_ref[0:depth] = state_ref[0:depth]
     up_ref[0:depth] = state_ref[pl.ds(size - depth, depth)]
     if forcing_ref is not None:
-        down_ref[depth:] = forcing_ref[0:STEPS]
-        up_ref[depth:] = forcing_ref[pl.ds(size - STEPS, STEPS)]
+        down_ref[depth : depth + STEPS] = forcing_ref[0:STEPS]
+        up_ref[depth : depth + STEPS] = forcing_ref[pl.ds(size - STEPS, STEPS)]
 
 
 def spread_kernel(size_ref, first_ref, own_ref, next_ref, up_ref, down_ref, rates_ref):
@@ -72,9 +68,36 @@
             at = (z * nx + x) * part
             own_ref[:, at : at + part, :] = first_ref[x, z, 0:WIDE]
             next_ref[:, at : at + part, :] = first_ref[x, z, WIDE : 2 * WIDE]
-            for s in range(rows - 2 * WIDE):
-                rates_ref[s, at : at + part, :] = first_ref[x, z, 2 * WIDE + s]
+            packed = first_ref[x, z, 2 * WIDE]
+            for s in range(1, rows - 2 * WIDE):
+                packed = packed + pltpu.roll(first_ref[x, z, 2 * WIDE + s], 2 * WIDE * s, 1)
+            rates_ref[at : at + part, :] = packed
     edges(size_ref[0], up_ref, down_ref, own_ref, next_ref)
+    down_ref[REACH + STEPS] = rates_ref[...]
+    up_ref[REACH + STEPS] = rates_ref[...]
+
+
+def widen_rates(out_ref, size_ref, own, low, high):
+    shape = own.shape
+    lanes = shape[1]
+    size, size_low = size_ref[0], size_ref[2]
+    lane = lax.broadcasted_iota(jnp.int32, shape, 1)
+    first = lane < LANE_B
+    place = jnp.where(first, lane, lane - LANE_B)
+
+    def moved(value, base, shift):
+        east = pltpu.roll(value, lax.rem(shift - base + 2 * lanes, lanes), 1)
+        north = pltpu.roll(value, lax.rem(shift + LANE_B - WIDE - base + 2 * lanes, lanes), 1)
+        return jnp.where(first, east, north)
+
+    for s in range(out_ref.shape[0]):
+        base = jnp.int32(2 * WIDE * s)
+        below = moved(low, base, REACH - size_low)
+        within = moved(own, base, jnp.int32(REACH))
+        above = moved(high, base, REACH + size)
+        out_ref[s] = jnp.where(
+            place < REACH, below, jnp.where(place < REACH + size, within, above)
+        )
 
 
 def fill_window(window, reach, size, own, low, high):
@@ -145,7 +168,10 @@
     coefficients = scratch[4:]
     size, x_place = size_ref[0], size_ref[1]
     fill_window(ping, REACH, size, own_ref[...], low_ref[0:REACH], high_ref[0:REACH])
-    fill_window(force, STEPS, size, mid_ref[...], low_ref[REACH:], high_ref[REACH:])
+    fill_window(
+        force, STEPS, size, mid_ref[...], low_ref[REACH : REACH + STEPS],
+        high_ref[REACH : REACH + STEPS],
+    )
     fill_table(table, mix_ref)
     rows = WIDE + 2 * REACH
     advance((ping, pong), 0, rows, 0, rates[0], coefficients, table)
@@ -157,9 +183,11 @@
 
 
 def early_kernel(
-    size_ref, own_ref, mid_ref, low_ref, high_ref, rates_ref, mix_ref, later_ref,
-    next_ref, mid_next_ref, end_next_ref, up_ref, down_ref, part_a, part_b, *scratch,
+    size_ref, own_ref, mid_ref, low_ref, high_ref, packed_ref, mix_ref, later_ref,
+    next_ref, mid_next_ref, end_next_ref, up_ref, down_ref, part_a, part_b, rates_ref, *scratch,
 ):
+    at = REACH + STEPS
+    widen_rates(rates_ref, size_ref, packed_ref[...], low_ref[at], high_ref[at])
     gather_x(next_ref, later_ref, 0)
     gather_x(mid_next_ref, later_ref, 1)
     gather_x(end_next_ref, later_ref, 2)
@@ -218,30 +246,38 @@
 
 
 def observe_kernel(
-    planes, odd_ref, strips_ref, forcing_ref, table_ref, state_ref, out_ref, turned, split
+    planes, odd_ref, strips_ref, forcing_ref, table_ref, state_ref, out_ref,
+    turned, split, tables, arrived,
 ):
     levels, width_x, width_y = forcing_ref.shape
-
-    @pl.when(pl.program_id(0) == 0)
-    def _():
-        odd = odd_ref[0]
-        starts = starts_of(width_y, planes)
-        for j in range(planes):
-            place = jnp.where(odd == 1, planes - 1 - j, j)
-            turned[starts[j] : starts[j] + WIDE] = strips_ref[place]
-        for x in range(width_x):
-            value = turned[:, x, :].T + forcing_ref[:, x, :]
-            state_ref[:, x, :] = value
-            high, low = halves(value)
-            split[0:levels, x * width_y : (x + 1) * width_y] = high
-            split[levels:, x * width_y : (x + 1) * width_y] = low
-
-    capacity = out_ref.shape[2]
-    for owner in range(out_ref.shape[0]):
-        both = jnp.dot(split[...], table_ref[owner], preferred_element_type=jnp.float32)
+    owners, _, capacity = out_ref.shape
+
+    def fetch(owner):
+        return pltpu.make_async_copy(table_ref.at[owner], tables.at[owner], arrived.at[owner])
+
+    for owner in range(owners):
+        fetch(owner).start()
+    odd = odd_ref[0]
+    starts = starts_of(width_y, planes)
+    for j in range(planes):
+        place = jnp.where(odd == 1, planes - 1 - j, j)
+        turned[starts[j] : starts[j] + WIDE] = strips_ref[place]
+    for x in range(width_x):
+        value = turned[:, x, :].T + forcing_ref[:, x, :]
+        state_ref[:, x, :] = value
+        high, low = halves(value)
+        split[0:levels, x * width_y : (x + 1) * width_y] = high
+        split[levels:, x * width_y : (x + 1) * width_y] = low
+
+    def observe(owner, carry):
+        fetch(owner).wait()
+        both = jnp.dot(split[...], tables[owner], preferred_element_type=jnp.float32)
         out_ref[owner] = both[:levels, :capacity] + (
             both[:levels, capacity:] + both[levels:, :capacity]
         )
+        return carry
+
+    lax.fori_loop(0, owners, observe, 0)
 
 
 def channel_kernel(table_ref, profile_ref, out_ref):
@@ -280,7 +316,9 @@
     strip = jnp.where(odd == 1, planes - 1 - place_z, place_z)
     size = (width_y * (strip + 1)) // planes - (width_y * strip) // planes
     odd = odd.reshape(1)
-    sizes = jnp.stack([size.astype(jnp.int32), lax.axis_index("x").astype(jnp.int32)])
+    below = jnp.where(strip == 0, planes - 1, strip - 1)
+    size_low = (width_y * (below + 1)) // planes - (width_y * below) // planes
+    sizes = jnp.stack([x.astype(jnp.int32) for x in (size, lax.axis_index("x"), size_low)])
 
     order = []
     for o in range(owners):
@@ -291,24 +329,19 @@
     chain = ("slot", "zhi", "obs")
 
     rates = winds[:, 0]
-    ring = [(i, (i + 1) % owners) for i in range(owners)]
-    back = [(target, source) for source, target in ring]
-    rates_low = lax.ppermute(rates[:, :, width_y - REACH :], "obs", ring)
-    rates_high = lax.ppermute(rates[:, :, :REACH], "obs", back)
-    around = jnp.concatenate(
-        [rates_high, jnp.zeros((2, width_x, width_y - 2 * REACH), jnp.float32), rates_low], axis=2
-    )
-
+    block_far, rates_far = (
+        pltpu.with_memory_space_constraint(x, pltpu.HBM) for x in (block, rates)
+    )
     cut = pl.pallas_call(
         functools.partial(cut_kernel, planes),
         out_shape=f32(planes, WIDE + 1, width_x, levels),
-        in_specs=[SMEM()] + [VMEM()] * 3,
+        in_specs=[SMEM(), VMEM(), VMEM()],
         out_specs=VMEM(),
         scratch_shapes=[pltpu.VMEM((width_y, width_x, levels), jnp.float32)],
         compiler_params=params(8),
         cost_estimate=cost(4000000, 1100000),
         name="cut",
-    )(odd, block, rates, around)
+    )(odd, block_far, rates_far)
     strips = lax.all_to_all(cut, ("zhi", "slot"), 0, 0, tiled=True)
     strips = strips.reshape(halves_z, slots, WIDE + 1, width_x, levels)
     first = jnp.concatenate(
@@ -325,11 +358,12 @@
     strip = f32(WIDE, whole_x, levels)
     far = pltpu.HBM((WIDE, whole_x, levels), jnp.float32)
     edge = f32(REACH + STEPS, whole_x, levels)
+    first_edge = f32(REACH + STEPS + 1, whole_x, levels)
     last_edge = f32(STEPS, whole_x, levels)
     part = f32(halves_z, WIDE, width_x, levels)
     own, mid, up, down, rates = pl.pallas_call(
         spread_kernel,
-        out_shape=(far, far, edge, edge, f32(rounds, whole_x, levels)),
+        out_shape=(far, far, first_edge, first_edge, f32(whole_x, levels)),
         in_specs=[SMEM(), VMEM()],
         out_specs=(VMEM(),) * 5,
         compiler_params=params(8),
@@ -351,11 +385,11 @@
     low = lax.ppermute(up, chain, upward)
     high = lax.ppermute(down, chain, downward)
     own, mid = (pltpu.with_memory_space_constraint(x, pltpu.HBM) for x in (own, mid))
-    own, mid, end, up, down, *kept = pl.pallas_call(
+    own, mid, end, up, down, *kept, rates = pl.pallas_call(
         early_kernel,
-        out_shape=(strip, strip, strip, edge, edge, part, part),
+        out_shape=(strip, strip, strip, edge, edge, part, part, f32(rounds, whole_x, levels)),
         in_specs=[SMEM()] + [VMEM()] * 7,
-        out_specs=(VMEM(),) * 7,
+        out_specs=(VMEM(),) * 8,
         scratch_shapes=long_scratch,
         compiler_params=params(24),
         cost_estimate=cost(900000000, 4000000),
@@ -411,20 +445,13 @@
     state, profile = pl.pallas_call(
         functools.partial(observe_kernel, planes),
         out_shape=(f32(levels, width_x, width_y), f32(owners, levels, capacity)),
-        grid=(owners // group,),
-        in_specs=[
-            SMEM(),
-            pl.BlockSpec((planes, WIDE, width_x, levels), lambda q: (0, 0, 0, 0)),
-            pl.BlockSpec((levels, width_x, width_y), lambda q: (0, 0, 0)),
-            pl.BlockSpec((group, columns, 2 * capacity), lambda q: (q, 0, 0)),
-        ],
-        out_specs=(
-            pl.BlockSpec((levels, width_x, width_y), lambda q: (0, 0, 0)),
-            pl.BlockSpec((group, levels, capacity), lambda q: (q, 0, 0)),
-        ),
+        in_specs=[SMEM(), VMEM(), VMEM(), pl.BlockSpec(memory_space=pltpu.HBM)],
+        out_specs=(VMEM(), VMEM()),
         scratch_shapes=[
             pltpu.VMEM((width_y, width_x, levels), jnp.float32),
             pltpu.VMEM((2 * levels, columns), jnp.bfloat16),
+            pltpu.VMEM((owners, columns, 2 * capacity), jnp.bfloat16),
+            pltpu.SemaphoreType.DMA((owners,)),
         ],
         compiler_params=params(20),
         cost_estimate=cost(2000000000, 11000000),

time: 201 us -> 194 us (0.965)
  starting transfers between devices: 48.3 us -> 32.2 us
  blocking collectives: 69.3 us -> 80.6 us
  local copies, waits for them, and re-layouts: 4.88 us -> 2.21 us
    all_to_all x1, blocking collectives: 28.8 us -> 40.8 us  [local(): strips = lax.all_to_all(cut, ('zhi', 'slot'), 0, 0, tiled=True)]
    ppermute x2 -> x0, starting transfers between devices: 10.5 us -> none  [the longest x1 10.5 us: local(): rates_high = lax.ppermute(rates[:, :, :REACH], 'obs', back)]
    ppermute x3, starting transfers between devices: 20.7 us -> 14.4 us  [local(): low = lax.ppermute(up, chain, upward)]
  transfers between devices with their start and end apart: 11 -> 9, of which waited for: 9 -> 9; matrix products, arithmetic and copies ran while one was open for 0% -> 0% of each run, Pallas kernels for 4% -> 5%
where the time goes in v3:
time: 194 us
  blocking collectives  80.6 us (42%)
  waiting for transfers between devices  46.3 us (24%)
  starting transfers between devices  32.2 us (17%)
  Pallas kernels  31.3 us (16%)
  local copies, waits for them, and re-layouts  2.21 us (1%)
    all_to_all x1, blocking collectives, local(): strips = lax.all_to_all(cut, ('zhi', 'slot'), 0, 0, tiled=True)  40.8 us
    all_to_all x1, blocking collectives, local(): profile = lax.all_to_all(profile, 'obs', 0, 0, tiled=True)  39.7 us
    ppermute x3, starting transfers between devices, local(): low = lax.ppermute(up, chain, upward)  14.4 us
    all_to_all x1, waiting for transfers between devices, local(): home = lax.all_to_all(home, ('zhi', 'slot'), 0, 0, tiled=True)  14.4 us
    ppermute x3, waiting for transfers between devices, local(): high = lax.ppermute(down, chain, downward)  13.9 us
    all_to_all x1, waiting for transfers between devices, local(): lax.all_to_all(jnp.broadcast_to(first, (parts_x,) + first.shape), 'x', 0,...  10.3 us
    pallas_call x1, Pallas kernels, local(): pl.pallas_call(table_kernel, out_shape=pltpu.HBM((owners, columns, 2 * ca...  7.27 us
    pallas_call x1, Pallas kernels, local(): pl.pallas_call(functools.partial(observe_kernel, planes), out_shape=(f32(...  7.15 us
  transfers between devices with their start and end apart: 9, of which 9 were waited for; matrix products, arithmetic and copies ran while one was open for 0% of the time, Pallas kernels for 5%

profile of v3, /device:TPU:1, one launch (start us, length us, event | category | flops | bytes accessed | tf_op | source)
XLA Modules:
  0.0 193.7 jit_solution(1388231498694762407)
XLA Ops:
  0.6 1.7 cut.1
  2.3 40.8 %all_to_all.25 = f32[12,12,8,128]{3,2,1,0:T(8,128)S(1)} all-to-all(f32[12,12,8,128]{3,2,1,0:T(8,128)S(1)} %cut.1), channel_id=1, replica_groups=mesh['slot'=6,'zhi'=2,'x'=4,'obs'=16] {'zhi','slot'}, dimensions={0} | all-to-all | bytes 1179648 | tf_op jit(solution)/shard_map/all_to_all | solution.py:345
  43.2 1.0 broadcast_in_dim.24
  44.2 4.0 %all-to-all-start.1 = ((f32[4,2,27,8,128]{4,3,2,1,0:T(8,128)}), f32[4,2,27,8,128]{4,3,2,1,0:T(8,128)S(1)}, u32[]{:S(2)}, u32[]{:S(2)}) async-start(f32[4,2,27,8,128]{4,3,2,1,0:T(8,128)} %broadcast_in_dim.24), calls=%async_computation.1 | async-start | bytes 1769472 | tf_op jit(solution)/shard_map/all_to_all | solution.py:351
  48.2 10.3 %all-to-all-done.1.first_ref = f32[4,2,27,8,128]{4,3,2,1,0:T(8,128)S(1)} async-done(((f32[4,2,27,8,128]{4,3,2,1,0:T(8,128)}), f32[4,2,27,8,128]{4,3,2,1,0:T(8,128)S(1)}, u32[]{:S(2)}, u32[]{:S(2)}) %all-to-all-start.1) | async-done | bytes 884768 | tf_op jit(solution)/shard_map/all_to_all | solution.py:351
  58.6 1.1 broadcast_in_dim.25
  59.6 3.6 %all-to-all-start.2 = ((f32[4,2,3,11,8,128]{5,4,3,2,1,0:T(8,128)}), f32[4,2,3,11,8,128]{5,4,3,2,1,0:T(8,128)S(1)}, u32[]{:S(2)}, u32[]{:S(2)}) async-start(f32[4,2,3,11,8,128]{5,4,3,2,1,0:T(8,128)} %broadcast_in_dim.25), calls=%async_computation.2 | async-start | bytes 2162688 | tf_op jit(solution)/shard_map/all_to_all | solution.py:354
  63.4 0.1 pad_add_fusion.size_ref
  63.5 1.5 spread.1
  64.9 7.0 %collective-permute-start = (f32[13,64,128]{2,1,0:T(8,128)S(1)}, f32[13,64,128]{2,1,0:T(8,128)S(1)}, u32[]{:S(2)}, u32[]{:S(2)}) collective-permute-start(f32[13,64,128]{2,1,0:T(8,128)S(1)} %get-tuple-element.26), channel_id=1, source_target_pairs={{15,0},{0,128},{128,256},{256,384},{384,512},{512,640},{640,64},{6... | collective-permute-start | bytes 1277960 | tf_op jit(solution)/shard_map/ppermute | solution.py:385
  71.9 2.0 %collective-permute-start.1 = (f32[13,64,128]{2,1,0:T(8,128)S(1)}, f32[13,64,128]{2,1,0:T(8,128)S(1)}, u32[]{:S(2)}, u32[]{:S(2)}) collective-permute-start(f32[13,64,128]{2,1,0:T(8,128)S(1)} %get-tuple-element.27), channel_id=1, source_target_pairs={{0,15},{128,0},{256,128},{384,256},{512,384},{640,512},{64,640},{1... | collective-permute-start | bytes 1277960 | tf_op jit(solution)/shard_map/ppermute | solution.py:386
  73.9 0.1 copy.10
  74.0 0.6 all-to-all-done.2.later_ref
  74.6 3.2 %collective-permute-done.low_ref = f32[13,64,128]{2,1,0:T(8,128)S(1)} collective-permute-done((f32[13,64,128]{2,1,0:T(8,128)S(1)}, f32[13,64,128]{2,1,0:T(8,128)S(1)}, u32[]{:S(2)}, u32[]{:S(2)}) %collective-permute-start) | collective-permute-done | bytes 426016 | tf_op jit(solution)/shard_map/ppermute | solution.py:385
  77.8 5.5 %collective-permute-done.1.high_ref = f32[13,64,128]{2,1,0:T(8,128)S(1)} collective-permute-done((f32[13,64,128]{2,1,0:T(8,128)S(1)}, f32[13,64,128]{2,1,0:T(8,128)S(1)}, u32[]{:S(2)}, u32[]{:S(2)}) %collective-permute-start.1) | collective-permute-done | bytes 426016 | tf_op jit(solution)/shard_map/ppermute | solution.py:386
  83.3 5.1 %early.1 = (f32[11,64,128]{2,1,0:T(8,128)S(1)}, f32[11,64,128]{2,1,0:T(8,128)S(1)}, f32[11,64,128]{2,1,0:T(8,128)S(1)}, f32[12,64,128]{2,1,0:T(8,128)S(1)}, f32[...) custom-call(s32[3]{0:T(128)S(1)} %pad_add_fusion.size_ref, ...), custom_call_target="tpu_custom_call" | custom-call | flops 900000000 | bytes 4000000 | tf_op jit(solution)/shard_map/early/pallas_call | solution.py:388
  88.4 3.8 %collective-permute-start.2 = (f32[12,64,128]{2,1,0:T(8,128)S(1)}, f32[12,64,128]{2,1,0:T(8,128)S(1)}, u32[]{:S(2)}, u32[]{:S(2)}) collective-permute-start(f32[12,64,128]{2,1,0:T(8,128)S(1)} %get-tuple-element.31), channel_id=1, source_target_pairs={{15,0},{0,128},{128,256},{256,384},{384,512},{512,640},{640,64},{6... | collective-permute-start | bytes 1179656 | tf_op jit(solution)/shard_map/ppermute | solution.py:398
  92.2 2.3 %collective-permute-start.3 = (f32[12,64,128]{2,1,0:T(8,128)S(1)}, f32[12,64,128]{2,1,0:T(8,128)S(1)}, u32[]{:S(2)}, u32[]{:S(2)}) collective-permute-start(f32[12,64,128]{2,1,0:T(8,128)S(1)} %get-tuple-element.32), channel_id=1, source_target_pairs={{0,15},{128,0},{256,128},{384,256},{512,384},{640,512},{64,640},{1... | collective-permute-start | bytes 1179656 | tf_op jit(solution)/shard_map/ppermute | solution.py:399
  94.5 3.4 %collective-permute-done.2.low_ref = f32[12,64,128]{2,1,0:T(8,128)S(1)} collective-permute-done((f32[12,64,128]{2,1,0:T(8,128)S(1)}, f32[12,64,128]{2,1,0:T(8,128)S(1)}, u32[]{:S(2)}, u32[]{:S(2)}) %collective-permute-start.2) | collective-permute-done | bytes 393248 | tf_op jit(solution)/shard_map/ppermute | solution.py:398
  97.9 4.6 %collective-permute-done.3.high_ref = f32[12,64,128]{2,1,0:T(8,128)S(1)} collective-permute-done((f32[12,64,128]{2,1,0:T(8,128)S(1)}, f32[12,64,128]{2,1,0:T(8,128)S(1)}, u32[]{:S(2)}, u32[]{:S(2)}) %collective-permute-start.3) | collective-permute-done | bytes 393248 | tf_op jit(solution)/shard_map/ppermute | solution.py:399
  102.5 4.4 %middle.1 = (f32[11,64,128]{2,1,0:T(8,128)S(1)}, f32[4,64,128]{2,1,0:T(8,128)S(1)}, f32[4,64,128]{2,1,0:T(8,128)S(1)}, f32[2,11,8,128]{3,2,1,0:T(8,128)S(1)}, f32[2,11,8,128]{3,2,1,0:T(8,128)S(1)}) custom-call(s32[3]{0:T(128)S(1)} %pad_add_fusion.size_ref, f32[11,64,128]{2,1,0:T(8,128)S(1)} %get-tuple-element.29.own_ref, ...), custom_call_target="tpu_custom_call" | custom-call | flops 900000000 | bytes 4000000 | tf_op jit(solution)/shard_map/middle/pallas_call | solution.py:400
  106.9 3.7 %collective-permute-start.4 = (f32[4,64,128]{2,1,0:T(8,128)S(1)}, f32[4,64,128]{2,1,0:T(8,128)S(1)}, u32[]{:S(2)}, u32[]{:S(2)}) collective-permute-start(f32[4,64,128]{2,1,0:T(8,128)S(1)} %get-tuple-element.36), channel_id=1, source_target_pairs={{15,0},{0,128},{128,256},{256,384},{384,512},{512,640},{640,64},{6... | collective-permute-start | bytes 393224 | tf_op jit(solution)/shard_map/ppermute | solution.py:410
  110.5 2.2 %collective-permute-start.5 = (f32[4,64,128]{2,1,0:T(8,128)S(1)}, f32[4,64,128]{2,1,0:T(8,128)S(1)}, u32[]{:S(2)}, u32[]{:S(2)}) collective-permute-start(f32[4,64,128]{2,1,0:T(8,128)S(1)} %get-tuple-element.37), channel_id=1, source_target_pairs={{0,15},{128,0},{256,128},{384,256},{512,384},{640,512},{64,640},{1... | collective-permute-start | bytes 393224 | tf_op jit(solution)/shard_map/ppermute | solution.py:411
  112.8 0.5 collective-permute-done.4.low_ref
  113.3 3.8 %collective-permute-done.5.high_ref = f32[4,64,128]{2,1,0:T(8,128)S(1)} collective-permute-done((f32[4,64,128]{2,1,0:T(8,128)S(1)}, f32[4,64,128]{2,1,0:T(8,128)S(1)}, u32[]{:S(2)}, u32[]{:S(2)}) %collective-permute-start.5) | collective-permute-done | bytes 131104 | tf_op jit(solution)/shard_map/ppermute | solution.py:411
  117.1 2.9 %late.1 = f32[2,6,11,8,128]{4,3,2,1,0:T(8,128)} custom-call(s32[3]{0:T(128)S(1)} %pad_add_fusion.size_ref, f32[11,64,128]{2,1,0:T(8,128)S(1)} %get-tuple-element.35.own_ref, f32[4,64,128]{2,1,0:T(8,128)S(1)} %collective-permute-done.4.low_ref, f32[4,64,128]{2,1,0:T(8,128)S(1)} %collective-permute-done.5.high_ref, ...), custom_call_target="tpu_custom_call" | custom-call | flops 400000000 | bytes 3000000 | tf_op jit(solution)/shard_map/late/pallas_call | solution.py:412
  120.0 3.6 %all-to-all-start.3 = ((f32[12,11,8,128]{3,2,1,0:T(8,128)}), f32[12,11,8,128]{3,2,1,0:T(8,128)S(1)}, u32[]{:S(2)}, u32[]{:S(2)}) async-start(f32[12,11,8,128]{3,2,1,0:T(8,128)} %bitcast.13), calls=%async_computation.3 | async-start | bytes 1081344 | tf_op jit(solution)/shard_map/all_to_all | solution.py:430
  123.7 7.3 %table.1.table_ref = bf16[16,1024,256]{2,1,0:T(8,128)(2,1)} custom-call(s32[4,2048]{1,0:T(4,128)S(1)} %bitcast.33, f32[4,2048]{1,0:T(4,128)S(1)} %bitcast_select_fusion.weights_ref), custom_call_target="tpu_custom_call" | custom-call | flops 1000000000 | bytes 8500000 | tf_op jit(solution)/shard_map/table/pallas_call | solution.py:434
  130.9 14.4 %all-to-all-done.3.strips_ref = f32[12,11,8,128]{3,2,1,0:T(8,128)S(1)} async-done(((f32[12,11,8,128]{3,2,1,0:T(8,128)}), f32[12,11,8,128]{3,2,1,0:T(8,128)S(1)}, u32[]{:S(2)}, u32[]{:S(2)}) %all-to-all-start.3) | async-done | bytes 540704 | tf_op jit(solution)/shard_map/all_to_all | solution.py:430
  145.4 7.1 %observe.1 = (f32[128,8,128]{2,1,0:T(8,128)}, f32[16,128,128]{2,1,0:T(8,128)S(1)}) custom-call(s32[1]{0:T(128)} %bitcast.odd_ref, f32[12,11,8,128]{3,2,1,0:T(8,128)S(1)} %all-to-all-done.3.strips_ref, f32[128,8,128]{2,1,0:T(8,128)S(1)} %bitcast.29, bf16[16,1024,256]{2,1,0:T(8,128)(2,1)} %table.1.table_ref), custom_call_target="tpu_custom_call" | custom-call | flops 2000000000 | bytes 11000000 | tf_op jit(solution)/shard_map/observe/pallas_call | solution.py:445
  152.5 39.7 %all_to_all.26.profile_ref = f32[16,128,128]{2,1,0:T(8,128)S(1)} all-to-all(f32[16,128,128]{2,1,0:T(8,128)S(1)} %get-tuple-element.45), channel_id=1, replica_groups=mesh['slot'=6,'zhi'=2,'x'=4,'obs'=16] {'obs'}, dimensions={0} | all-to-all | bytes 2097152 | tf_op jit(solution)/shard_map/all_to_all | solution.py:461
  192.2 1.4 channel.1
  (19 shorter events, 0.2 us)
Async XLA Ops:
  44.2 14.4 %all-to-all-start.1 = ((f32[4,2,27,8,128]{4,3,2,1,0:T(8,128)}), f32[4,2,27,8,128]{4,3,2,1,0:T(8,128)S(1)}, u32[]{:S(2)}, u32[]{:S(2)}) async-start(f32[4,2,27,8,128]{4,3,2,1,0:T(8,128)} %broadcast_in_dim.24), calls=%async_computation.1 | async-start | bytes 1769472 | tf_op jit(solution)/shard_map/all_to_all | solution.py:351
  59.6 14.3 %copy-start.2 = (f32[128,128]{1,0:T(8,128)S(1)}, f32[128,128]{1,0:T(8,128)}, u32[]{:S(2)}) copy-start(f32[128,128]{1,0:T(8,128)} %param.9) | copy-start | bytes 196612
  59.6 14.9 %all-to-all-start.2 = ((f32[4,2,3,11,8,128]{5,4,3,2,1,0:T(8,128)}), f32[4,2,3,11,8,128]{5,4,3,2,1,0:T(8,128)S(1)}, u32[]{:S(2)}, u32[]{:S(2)}) async-start(f32[4,2,3,11,8,128]{5,4,3,2,1,0:T(8,128)} %broadcast_in_dim.25), calls=%async_computation.2 | async-start | bytes 2162688 | tf_op jit(solution)/shard_map/all_to_all | solution.py:354
  64.9 12.8 %collective-permute-start = (f32[13,64,128]{2,1,0:T(8,128)S(1)}, f32[13,64,128]{2,1,0:T(8,128)S(1)}, u32[]{:S(2)}, u32[]{:S(2)}) collective-permute-start(f32[13,64,128]{2,1,0:T(8,128)S(1)} %get-tuple-element.26), channel_id=1, source_target_pairs={{15,0},{0,128},{128,256},{256,384},{384,512},{512,640},{640,64},{6... | collective-permute-start | bytes 1277960 | tf_op jit(solution)/shard_map/ppermute | solution.py:385
  71.9 11.4 %collective-permute-start.1 = (f32[13,64,128]{2,1,0:T(8,128)S(1)}, f32[13,64,128]{2,1,0:T(8,128)S(1)}, u32[]{:S(2)}, u32[]{:S(2)}) collective-permute-start(f32[13,64,128]{2,1,0:T(8,128)S(1)} %get-tuple-element.27), channel_id=1, source_target_pairs={{0,15},{128,0},{256,128},{384,256},{512,384},{640,512},{64,640},{1... | collective-permute-start | bytes 1277960 | tf_op jit(solution)/shard_map/ppermute | solution.py:386
  83.3 11.1 %copy-start.5 = (s32[1,1,16]{2,1,0:T(1,128)S(1)}, s32[1,1,16]{2,1,0:T(1,128)}, u32[]{:S(2)}) copy-start(s32[1,1,16]{2,1,0:T(1,128)} %param.12) | copy-start | bytes 196
  88.4 9.6 %collective-permute-start.2 = (f32[12,64,128]{2,1,0:T(8,128)S(1)}, f32[12,64,128]{2,1,0:T(8,128)S(1)}, u32[]{:S(2)}, u32[]{:S(2)}) collective-permute-start(f32[12,64,128]{2,1,0:T(8,128)S(1)} %get-tuple-element.31), channel_id=1, source_target_pairs={{15,0},{0,128},{128,256},{256,384},{384,512},{512,640},{640,64},{6... | collective-permute-start | bytes 1179656 | tf_op jit(solution)/shard_map/ppermute | solution.py:398
  92.2 10.3 %collective-permute-start.3 = (f32[12,64,128]{2,1,0:T(8,128)S(1)}, f32[12,64,128]{2,1,0:T(8,128)S(1)}, u32[]{:S(2)}, u32[]{:S(2)}) collective-permute-start(f32[12,64,128]{2,1,0:T(8,128)S(1)} %get-tuple-element.32), channel_id=1, source_target_pairs={{0,15},{128,0},{256,128},{384,256},{512,384},{640,512},{64,640},{1... | collective-permute-start | bytes 1179656 | tf_op jit(solution)/shard_map/ppermute | solution.py:399
  102.5 10.3 %copy-start.3 = (f32[4,1,2048]{2,1,0:T(1,128)S(1)}, f32[4,1,2048]{2,1,0:T(1,128)}, u32[]{:S(2)}) copy-start(f32[4,1,2048]{2,1,0:T(1,128)} %param.11) | copy-start | bytes 98308
  106.9 6.5 %collective-permute-start.4 = (f32[4,64,128]{2,1,0:T(8,128)S(1)}, f32[4,64,128]{2,1,0:T(8,128)S(1)}, u32[]{:S(2)}, u32[]{:S(2)}) collective-permute-start(f32[4,64,128]{2,1,0:T(8,128)S(1)} %get-tuple-element.36), channel_id=1, source_target_pairs={{15,0},{0,128},{128,256},{256,384},{384,512},{512,640},{640,64},{6... | collective-permute-start | bytes 393224 | tf_op jit(solution)/shard_map/ppermute | solution.py:410
  110.5 6.6 %collective-permute-start.5 = (f32[4,64,128]{2,1,0:T(8,128)S(1)}, f32[4,64,128]{2,1,0:T(8,128)S(1)}, u32[]{:S(2)}, u32[]{:S(2)}) collective-permute-start(f32[4,64,128]{2,1,0:T(8,128)S(1)} %get-tuple-element.37), channel_id=1, source_target_pairs={{0,15},{128,0},{256,128},{384,256},{512,384},{640,512},{64,640},{1... | collective-permute-start | bytes 393224 | tf_op jit(solution)/shard_map/ppermute | solution.py:411
  117.1 6.5 %copy-start.4 = (s32[4,1,2048]{2,1,0:T(1,128)S(1)}, s32[4,1,2048]{2,1,0:T(1,128)}, u32[]{:S(2)}) copy-start(s32[4,1,2048]{2,1,0:T(1,128)} %param.10) | copy-start | bytes 98308
  120.0 25.3 %all-to-all-start.3 = ((f32[12,11,8,128]{3,2,1,0:T(8,128)}), f32[12,11,8,128]{3,2,1,0:T(8,128)S(1)}, u32[]{:S(2)}, u32[]{:S(2)}) async-start(f32[12,11,8,128]{3,2,1,0:T(8,128)} %bitcast.13), calls=%async_computation.3 | async-start | bytes 1081344 | tf_op jit(solution)/shard_map/all_to_all | solution.py:430
  123.7 21.7 %copy-start = (f32[1,128,8,128]{3,2,1,0:T(8,128)S(1)}, f32[1,128,8,128]{3,2,1,0:T(8,128)}, u32[]{:S(2)}) copy-start(f32[1,128,8,128]{3,2,1,0:T(8,128)} %param.7) | copy-start | bytes 1572868
  152.5 39.7 %copy-start.1 = (f32[1,1,128,128]{3,2,1,0:T(8,128)S(1)}, f32[1,1,128,128]{3,2,1,0:T(8,128)}, u32[]{:S(2)}) copy-start(f32[1,1,128,128]{3,2,1,0:T(8,128)} %param.13) | copy-start | bytes 196612

commit v4 on v3

--- a/solution.py
+++ b/solution.py
@@ -247,7 +247,7 @@
 
 def observe_kernel(
     planes, odd_ref, strips_ref, forcing_ref, table_ref, state_ref, out_ref,
-    turned, split, tables, arrived,
+    turned, split, tables, state, arrived, sent,
 ):
     levels, width_x, width_y = forcing_ref.shape
     owners, _, capacity = out_ref.shape
@@ -264,20 +264,28 @@
         turned[starts[j] : starts[j] + WIDE] = strips_ref[place]
     for x in range(width_x):
         value = turned[:, x, :].T + forcing_ref[:, x, :]
-        state_ref[:, x, :] = value
+        state[:, x, :] = value
         high, low = halves(value)
         split[0:levels, x * width_y : (x + 1) * width_y] = high
         split[levels:, x * width_y : (x + 1) * width_y] = low
-
-    def observe(owner, carry):
-        fetch(owner).wait()
-        both = jnp.dot(split[...], tables[owner], preferred_element_type=jnp.float32)
-        out_ref[owner] = both[:levels, :capacity] + (
-            both[:levels, capacity:] + both[levels:, :capacity]
-        )
+    group = 4
+
+    def observe(trip, carry):
+        for member in range(group):
+            fetch(trip * group + member).wait()
+        for member in range(group):
+            owner = trip * group + member
+            both = jnp.dot(split[...], tables[owner], preferred_element_type=jnp.float32)
+            out_ref[owner] = both[:levels, :capacity] + (
+                both[:levels, capacity:] + both[levels:, :capacity]
+            )
         return carry
 
-    lax.fori_loop(0, owners, observe, 0)
+    observe(0, 0)
+    leave = pltpu.make_async_copy(state, state_ref, sent)
+    leave.start()
+    lax.fori_loop(1, owners // group, observe, 0)
+    leave.wait()
 
 
 def channel_kernel(table_ref, profile_ref, out_ref):
@@ -446,12 +454,14 @@
         functools.partial(observe_kernel, planes),
         out_shape=(f32(levels, width_x, width_y), f32(owners, levels, capacity)),
         in_specs=[SMEM(), VMEM(), VMEM(), pl.BlockSpec(memory_space=pltpu.HBM)],
-        out_specs=(VMEM(), VMEM()),
+        out_specs=(pl.BlockSpec(memory_space=pltpu.HBM), VMEM()),
         scratch_shapes=[
             pltpu.VMEM((width_y, width_x, levels), jnp.float32),
             pltpu.VMEM((2 * levels, columns), jnp.bfloat16),
             pltpu.VMEM((owners, columns, 2 * capacity), jnp.bfloat16),
+            pltpu.VMEM((levels, width_x, width_y), jnp.float32),
             pltpu.SemaphoreType.DMA((owners,)),
+            pltpu.SemaphoreType.DMA,
         ],
         compiler_params=params(20),
         cost_estimate=cost(2000000000, 11000000),

time: 194 us -> 192 us (0.990)
  no operation moved by 1% of the time
where the time goes in v4:
time: 192 us
  blocking collectives  80.6 us (42%)
  waiting for transfers between devices  46.3 us (24%)
  starting transfers between devices  32.2 us (17%)
  Pallas kernels  29.4 us (15%)
  local copies, waits for them, and re-layouts  2.21 us (1%)
    all_to_all x1, blocking collectives, local(): strips = lax.all_to_all(cut, ('zhi', 'slot'), 0, 0, tiled=True)  40.8 us
    all_to_all x1, blocking collectives, local(): profile = lax.all_to_all(profile, 'obs', 0, 0, tiled=True)  39.7 us
    ppermute x3, starting transfers between devices, local(): low = lax.ppermute(up, chain, upward)  14.4 us
    all_to_all x1, waiting for transfers between devices, local(): home = lax.all_to_all(home, ('zhi', 'slot'), 0, 0, tiled=True)  14.4 us
    ppermute x3, waiting for transfers between devices, local(): high = lax.ppermute(down, chain, downward)  13.9 us
    all_to_all x1, waiting for transfers between devices, local(): lax.all_to_all(jnp.broadcast_to(first, (parts_x,) + first.shape), 'x', 0,...  10.3 us
    pallas_call x1, Pallas kernels, local(): pl.pallas_call(table_kernel, out_shape=pltpu.HBM((owners, columns, 2 * ca...  7.27 us
    ppermute x3, waiting for transfers between devices, local(): low = lax.ppermute(up, chain, upward)  7.12 us
  transfers between devices with their start and end apart: 9, of which 9 were waited for; matrix products, arithmetic and copies ran while one was open for 0% of the time, Pallas kernels for 5%

profile of v4, /device:TPU:1, one launch (start us, length us, event | category | flops | bytes accessed | tf_op | source)
XLA Modules:
  0.0 191.8 jit_solution(386738140438960086)
XLA Ops:
  0.6 1.7 cut.1
  2.3 40.8 %all_to_all.25 = f32[12,12,8,128]{3,2,1,0:T(8,128)S(1)} all-to-all(f32[12,12,8,128]{3,2,1,0:T(8,128)S(1)} %cut.1), channel_id=1, replica_groups=mesh['slot'=6,'zhi'=2,'x'=4,'obs'=16] {'zhi','slot'}, dimensions={0} | all-to-all | bytes 1179648 | tf_op jit(solution)/shard_map/all_to_all | solution.py:353
  43.2 1.0 broadcast_in_dim.24
  44.2 4.0 %all-to-all-start.1 = ((f32[4,2,27,8,128]{4,3,2,1,0:T(8,128)}), f32[4,2,27,8,128]{4,3,2,1,0:T(8,128)S(1)}, u32[]{:S(2)}, u32[]{:S(2)}) async-start(f32[4,2,27,8,128]{4,3,2,1,0:T(8,128)} %broadcast_in_dim.24), calls=%async_computation.1 | async-start | bytes 1769472 | tf_op jit(solution)/shard_map/all_to_all | solution.py:359
  48.2 10.3 %all-to-all-done.1.first_ref = f32[4,2,27,8,128]{4,3,2,1,0:T(8,128)S(1)} async-done(((f32[4,2,27,8,128]{4,3,2,1,0:T(8,128)}), f32[4,2,27,8,128]{4,3,2,1,0:T(8,128)S(1)}, u32[]{:S(2)}, u32[]{:S(2)}) %all-to-all-start.1) | async-done | bytes 884768 | tf_op jit(solution)/shard_map/all_to_all | solution.py:359
  58.6 1.1 broadcast_in_dim.25
  59.6 3.6 %all-to-all-start.2 = ((f32[4,2,3,11,8,128]{5,4,3,2,1,0:T(8,128)}), f32[4,2,3,11,8,128]{5,4,3,2,1,0:T(8,128)S(1)}, u32[]{:S(2)}, u32[]{:S(2)}) async-start(f32[4,2,3,11,8,128]{5,4,3,2,1,0:T(8,128)} %broadcast_in_dim.25), calls=%async_computation.2 | async-start | bytes 2162688 | tf_op jit(solution)/shard_map/all_to_all | solution.py:362
  63.4 0.1 pad_add_fusion.size_ref
  63.5 1.5 spread.1
  64.9 7.0 %collective-permute-start = (f32[13,64,128]{2,1,0:T(8,128)S(1)}, f32[13,64,128]{2,1,0:T(8,128)S(1)}, u32[]{:S(2)}, u32[]{:S(2)}) collective-permute-start(f32[13,64,128]{2,1,0:T(8,128)S(1)} %get-tuple-element.26), channel_id=1, source_target_pairs={{15,0},{0,128},{128,256},{256,384},{384,512},{512,640},{640,64},{6... | collective-permute-start | bytes 1277960 | tf_op jit(solution)/shard_map/ppermute | solution.py:393
  71.9 2.0 %collective-permute-start.1 = (f32[13,64,128]{2,1,0:T(8,128)S(1)}, f32[13,64,128]{2,1,0:T(8,128)S(1)}, u32[]{:S(2)}, u32[]{:S(2)}) collective-permute-start(f32[13,64,128]{2,1,0:T(8,128)S(1)} %get-tuple-element.27), channel_id=1, source_target_pairs={{0,15},{128,0},{256,128},{384,256},{512,384},{640,512},{64,640},{1... | collective-permute-start | bytes 1277960 | tf_op jit(solution)/shard_map/ppermute | solution.py:394
  73.9 0.1 copy.10
  74.0 0.6 all-to-all-done.2.later_ref
  74.6 3.2 %collective-permute-done.low_ref = f32[13,64,128]{2,1,0:T(8,128)S(1)} collective-permute-done((f32[13,64,128]{2,1,0:T(8,128)S(1)}, f32[13,64,128]{2,1,0:T(8,128)S(1)}, u32[]{:S(2)}, u32[]{:S(2)}) %collective-permute-start) | collective-permute-done | bytes 426016 | tf_op jit(solution)/shard_map/ppermute | solution.py:393
  77.8 5.5 %collective-permute-done.1.high_ref = f32[13,64,128]{2,1,0:T(8,128)S(1)} collective-permute-done((f32[13,64,128]{2,1,0:T(8,128)S(1)}, f32[13,64,128]{2,1,0:T(8,128)S(1)}, u32[]{:S(2)}, u32[]{:S(2)}) %collective-permute-start.1) | collective-permute-done | bytes 426016 | tf_op jit(solution)/shard_map/ppermute | solution.py:394
  83.3 5.1 %early.1 = (f32[11,64,128]{2,1,0:T(8,128)S(1)}, f32[11,64,128]{2,1,0:T(8,128)S(1)}, f32[11,64,128]{2,1,0:T(8,128)S(1)}, f32[12,64,128]{2,1,0:T(8,128)S(1)}, f32[...) custom-call(s32[3]{0:T(128)S(1)} %pad_add_fusion.size_ref, ...), custom_call_target="tpu_custom_call" | custom-call | flops 900000000 | bytes 4000000 | tf_op jit(solution)/shard_map/early/pallas_call | solution.py:396
  88.4 3.8 %collective-permute-start.2 = (f32[12,64,128]{2,1,0:T(8,128)S(1)}, f32[12,64,128]{2,1,0:T(8,128)S(1)}, u32[]{:S(2)}, u32[]{:S(2)}) collective-permute-start(f32[12,64,128]{2,1,0:T(8,128)S(1)} %get-tuple-element.31), channel_id=1, source_target_pairs={{15,0},{0,128},{128,256},{256,384},{384,512},{512,640},{640,64},{6... | collective-permute-start | bytes 1179656 | tf_op jit(solution)/shard_map/ppermute | solution.py:406
  92.2 2.3 %collective-permute-start.3 = (f32[12,64,128]{2,1,0:T(8,128)S(1)}, f32[12,64,128]{2,1,0:T(8,128)S(1)}, u32[]{:S(2)}, u32[]{:S(2)}) collective-permute-start(f32[12,64,128]{2,1,0:T(8,128)S(1)} %get-tuple-element.32), channel_id=1, source_target_pairs={{0,15},{128,0},{256,128},{384,256},{512,384},{640,512},{64,640},{1... | collective-permute-start | bytes 1179656 | tf_op jit(solution)/shard_map/ppermute | solution.py:407
  94.5 3.4 %collective-permute-done.2.low_ref = f32[12,64,128]{2,1,0:T(8,128)S(1)} collective-permute-done((f32[12,64,128]{2,1,0:T(8,128)S(1)}, f32[12,64,128]{2,1,0:T(8,128)S(1)}, u32[]{:S(2)}, u32[]{:S(2)}) %collective-permute-start.2) | collective-permute-done | bytes 393248 | tf_op jit(solution)/shard_map/ppermute | solution.py:406
  97.9 4.6 %collective-permute-done.3.high_ref = f32[12,64,128]{2,1,0:T(8,128)S(1)} collective-permute-done((f32[12,64,128]{2,1,0:T(8,128)S(1)}, f32[12,64,128]{2,1,0:T(8,128)S(1)}, u32[]{:S(2)}, u32[]{:S(2)}) %collective-permute-start.3) | collective-permute-done | bytes 393248 | tf_op jit(solution)/shard_map/ppermute | solution.py:407
  102.5 4.4 %middle.1 = (f32[11,64,128]{2,1,0:T(8,128)S(1)}, f32[4,64,128]{2,1,0:T(8,128)S(1)}, f32[4,64,128]{2,1,0:T(8,128)S(1)}, f32[2,11,8,128]{3,2,1,0:T(8,128)S(1)}, f32[2,11,8,128]{3,2,1,0:T(8,128)S(1)}) custom-call(s32[3]{0:T(128)S(1)} %pad_add_fusion.size_ref, f32[11,64,128]{2,1,0:T(8,128)S(1)} %get-tuple-element.29.own_ref, ...), custom_call_target="tpu_custom_call" | custom-call | flops 900000000 | bytes 4000000 | tf_op jit(solution)/shard_map/middle/pallas_call | solution.py:408
  106.9 3.7 %collective-permute-start.4 = (f32[4,64,128]{2,1,0:T(8,128)S(1)}, f32[4,64,128]{2,1,0:T(8,128)S(1)}, u32[]{:S(2)}, u32[]{:S(2)}) collective-permute-start(f32[4,64,128]{2,1,0:T(8,128)S(1)} %get-tuple-element.36), channel_id=1, source_target_pairs={{15,0},{0,128},{128,256},{256,384},{384,512},{512,640},{640,64},{6... | collective-permute-start | bytes 393224 | tf_op jit(solution)/shard_map/ppermute | solution.py:418
  110.5 2.2 %collective-permute-start.5 = (f32[4,64,128]{2,1,0:T(8,128)S(1)}, f32[4,64,128]{2,1,0:T(8,128)S(1)}, u32[]{:S(2)}, u32[]{:S(2)}) collective-permute-start(f32[4,64,128]{2,1,0:T(8,128)S(1)} %get-tuple-element.37), channel_id=1, source_target_pairs={{0,15},{128,0},{256,128},{384,256},{512,384},{640,512},{64,640},{1... | collective-permute-start | bytes 393224 | tf_op jit(solution)/shard_map/ppermute | solution.py:419
  112.8 0.5 collective-permute-done.4.low_ref
  113.3 3.8 %collective-permute-done.5.high_ref = f32[4,64,128]{2,1,0:T(8,128)S(1)} collective-permute-done((f32[4,64,128]{2,1,0:T(8,128)S(1)}, f32[4,64,128]{2,1,0:T(8,128)S(1)}, u32[]{:S(2)}, u32[]{:S(2)}) %collective-permute-start.5) | collective-permute-done | bytes 131104 | tf_op jit(solution)/shard_map/ppermute | solution.py:419
  117.1 2.9 %late.1 = f32[2,6,11,8,128]{4,3,2,1,0:T(8,128)} custom-call(s32[3]{0:T(128)S(1)} %pad_add_fusion.size_ref, f32[11,64,128]{2,1,0:T(8,128)S(1)} %get-tuple-element.35.own_ref, f32[4,64,128]{2,1,0:T(8,128)S(1)} %collective-permute-done.4.low_ref, f32[4,64,128]{2,1,0:T(8,128)S(1)} %collective-permute-done.5.high_ref, ...), custom_call_target="tpu_custom_call" | custom-call | flops 400000000 | bytes 3000000 | tf_op jit(solution)/shard_map/late/pallas_call | solution.py:420
  120.0 3.6 %all-to-all-start.3 = ((f32[12,11,8,128]{3,2,1,0:T(8,128)}), f32[12,11,8,128]{3,2,1,0:T(8,128)S(1)}, u32[]{:S(2)}, u32[]{:S(2)}) async-start(f32[12,11,8,128]{3,2,1,0:T(8,128)} %bitcast.13), calls=%async_computation.3 | async-start | bytes 1081344 | tf_op jit(solution)/shard_map/all_to_all | solution.py:438
  123.7 7.3 %table.1.table_ref = bf16[16,1024,256]{2,1,0:T(8,128)(2,1)} custom-call(s32[4,2048]{1,0:T(4,128)S(1)} %bitcast.33, f32[4,2048]{1,0:T(4,128)S(1)} %bitcast_select_fusion.weights_ref), custom_call_target="tpu_custom_call" | custom-call | flops 1000000000 | bytes 8500000 | tf_op jit(solution)/shard_map/table/pallas_call | solution.py:442
  130.9 14.4 %all-to-all-done.3.strips_ref = f32[12,11,8,128]{3,2,1,0:T(8,128)S(1)} async-done(((f32[12,11,8,128]{3,2,1,0:T(8,128)}), f32[12,11,8,128]{3,2,1,0:T(8,128)S(1)}, u32[]{:S(2)}, u32[]{:S(2)}) %all-to-all-start.3) | async-done | bytes 540704 | tf_op jit(solution)/shard_map/all_to_all | solution.py:438
  145.4 5.2 %observe.1 = (f32[128,8,128]{2,1,0:T(8,128)}, f32[16,128,128]{2,1,0:T(8,128)S(1)}) custom-call(s32[1]{0:T(128)} %bitcast.odd_ref, f32[12,11,8,128]{3,2,1,0:T(8,128)S(1)} %all-to-all-done.3.strips_ref, f32[128,8,128]{2,1,0:T(8,128)S(1)} %bitcast.29, bf16[16,1024,256]{2,1,0:T(8,128)(2,1)} %table.1.table_ref), custom_call_target="tpu_custom_call" | custom-call | flops 2000000000 | bytes 11000000 | tf_op jit(solution)/shard_map/observe/pallas_call | solution.py:453
  150.6 39.7 %all_to_all.26.profile_ref = f32[16,128,128]{2,1,0:T(8,128)S(1)} all-to-all(f32[16,128,128]{2,1,0:T(8,128)S(1)} %get-tuple-element.45), channel_id=1, replica_groups=mesh['slot'=6,'zhi'=2,'x'=4,'obs'=16] {'obs'}, dimensions={0} | all-to-all | bytes 2097152 | tf_op jit(solution)/shard_map/all_to_all | solution.py:471
  190.3 1.4 channel.1
  (19 shorter events, 0.2 us)
Async XLA Ops:
  44.2 14.4 %all-to-all-start.1 = ((f32[4,2,27,8,128]{4,3,2,1,0:T(8,128)}), f32[4,2,27,8,128]{4,3,2,1,0:T(8,128)S(1)}, u32[]{:S(2)}, u32[]{:S(2)}) async-start(f32[4,2,27,8,128]{4,3,2,1,0:T(8,128)} %broadcast_in_dim.24), calls=%async_computation.1 | async-start | bytes 1769472 | tf_op jit(solution)/shard_map/all_to_all | solution.py:359
  59.6 14.3 %copy-start.2 = (f32[128,128]{1,0:T(8,128)S(1)}, f32[128,128]{1,0:T(8,128)}, u32[]{:S(2)}) copy-start(f32[128,128]{1,0:T(8,128)} %param.9) | copy-start | bytes 196612
  59.6 14.9 %all-to-all-start.2 = ((f32[4,2,3,11,8,128]{5,4,3,2,1,0:T(8,128)}), f32[4,2,3,11,8,128]{5,4,3,2,1,0:T(8,128)S(1)}, u32[]{:S(2)}, u32[]{:S(2)}) async-start(f32[4,2,3,11,8,128]{5,4,3,2,1,0:T(8,128)} %broadcast_in_dim.25), calls=%async_computation.2 | async-start | bytes 2162688 | tf_op jit(solution)/shard_map/all_to_all | solution.py:362
  64.9 12.8 %collective-permute-start = (f32[13,64,128]{2,1,0:T(8,128)S(1)}, f32[13,64,128]{2,1,0:T(8,128)S(1)}, u32[]{:S(2)}, u32[]{:S(2)}) collective-permute-start(f32[13,64,128]{2,1,0:T(8,128)S(1)} %get-tuple-element.26), channel_id=1, source_target_pairs={{15,0},{0,128},{128,256},{256,384},{384,512},{512,640},{640,64},{6... | collective-permute-start | bytes 1277960 | tf_op jit(solution)/shard_map/ppermute | solution.py:393
  71.9 11.4 %collective-permute-start.1 = (f32[13,64,128]{2,1,0:T(8,128)S(1)}, f32[13,64,128]{2,1,0:T(8,128)S(1)}, u32[]{:S(2)}, u32[]{:S(2)}) collective-permute-start(f32[13,64,128]{2,1,0:T(8,128)S(1)} %get-tuple-element.27), channel_id=1, source_target_pairs={{0,15},{128,0},{256,128},{384,256},{512,384},{640,512},{64,640},{1... | collective-permute-start | bytes 1277960 | tf_op jit(solution)/shard_map/ppermute | solution.py:394
  83.3 11.1 %copy-start.5 = (s32[1,1,16]{2,1,0:T(1,128)S(1)}, s32[1,1,16]{2,1,0:T(1,128)}, u32[]{:S(2)}) copy-start(s32[1,1,16]{2,1,0:T(1,128)} %param.12) | copy-start | bytes 196
  88.4 9.6 %collective-permute-start.2 = (f32[12,64,128]{2,1,0:T(8,128)S(1)}, f32[12,64,128]{2,1,0:T(8,128)S(1)}, u32[]{:S(2)}, u32[]{:S(2)}) collective-permute-start(f32[12,64,128]{2,1,0:T(8,128)S(1)} %get-tuple-element.31), channel_id=1, source_target_pairs={{15,0},{0,128},{128,256},{256,384},{384,512},{512,640},{640,64},{6... | collective-permute-start | bytes 1179656 | tf_op jit(solution)/shard_map/ppermute | solution.py:406
  92.2 10.3 %collective-permute-start.3 = (f32[12,64,128]{2,1,0:T(8,128)S(1)}, f32[12,64,128]{2,1,0:T(8,128)S(1)}, u32[]{:S(2)}, u32[]{:S(2)}) collective-permute-start(f32[12,64,128]{2,1,0:T(8,128)S(1)} %get-tuple-element.32), channel_id=1, source_target_pairs={{0,15},{128,0},{256,128},{384,256},{512,384},{640,512},{64,640},{1... | collective-permute-start | bytes 1179656 | tf_op jit(solution)/shard_map/ppermute | solution.py:407
  102.5 10.3 %copy-start.3 = (f32[4,1,2048]{2,1,0:T(1,128)S(1)}, f32[4,1,2048]{2,1,0:T(1,128)}, u32[]{:S(2)}) copy-start(f32[4,1,2048]{2,1,0:T(1,128)} %param.11) | copy-start | bytes 98308
  106.9 6.5 %collective-permute-start.4 = (f32[4,64,128]{2,1,0:T(8,128)S(1)}, f32[4,64,128]{2,1,0:T(8,128)S(1)}, u32[]{:S(2)}, u32[]{:S(2)}) collective-permute-start(f32[4,64,128]{2,1,0:T(8,128)S(1)} %get-tuple-element.36), channel_id=1, source_target_pairs={{15,0},{0,128},{128,256},{256,384},{384,512},{512,640},{640,64},{6... | collective-permute-start | bytes 393224 | tf_op jit(solution)/shard_map/ppermute | solution.py:418
  110.5 6.6 %collective-permute-start.5 = (f32[4,64,128]{2,1,0:T(8,128)S(1)}, f32[4,64,128]{2,1,0:T(8,128)S(1)}, u32[]{:S(2)}, u32[]{:S(2)}) collective-permute-start(f32[4,64,128]{2,1,0:T(8,128)S(1)} %get-tuple-element.37), channel_id=1, source_target_pairs={{0,15},{128,0},{256,128},{384,256},{512,384},{640,512},{64,640},{1... | collective-permute-start | bytes 393224 | tf_op jit(solution)/shard_map/ppermute | solution.py:419
  117.1 6.5 %copy-start.4 = (s32[4,1,2048]{2,1,0:T(1,128)S(1)}, s32[4,1,2048]{2,1,0:T(1,128)}, u32[]{:S(2)}) copy-start(s32[4,1,2048]{2,1,0:T(1,128)} %param.10) | copy-start | bytes 98308
  120.0 25.3 %all-to-all-start.3 = ((f32[12,11,8,128]{3,2,1,0:T(8,128)}), f32[12,11,8,128]{3,2,1,0:T(8,128)S(1)}, u32[]{:S(2)}, u32[]{:S(2)}) async-start(f32[12,11,8,128]{3,2,1,0:T(8,128)} %bitcast.13), calls=%async_computation.3 | async-start | bytes 1081344 | tf_op jit(solution)/shard_map/all_to_all | solution.py:438
  123.7 21.7 %copy-start = (f32[1,128,8,128]{3,2,1,0:T(8,128)S(1)}, f32[1,128,8,128]{3,2,1,0:T(8,128)}, u32[]{:S(2)}) copy-start(f32[1,128,8,128]{3,2,1,0:T(8,128)} %param.7) | copy-start | bytes 1572868
  150.6 39.7 %copy-start.1 = (f32[1,1,128,128]{3,2,1,0:T(8,128)S(1)}, f32[1,1,128,128]{3,2,1,0:T(8,128)}, u32[]{:S(2)}) copy-start(f32[1,1,128,128]{3,2,1,0:T(8,128)} %param.13) | copy-start | bytes 196612
